TPU v7x, 32 devices: a whole 2x2x4 slice. The times are simulated.
32 devices in a mesh: psr: 8 (over z, x), toa: 4 (over y, core).
Axes of the slice: x: 2, y: 2, z: 4, core: 2. Of those that a mesh axis runs over, the one named last changes fastest.
Arguments:
- design: bfloat16 [3072, 128, 256], P(('psr', 'toa')), may hold values from -0.035888672 to 0.035888672
- noise_weight: float32 [3072, 128], P(('psr', 'toa')), may hold values from 0.3 to 3
- residuals: bfloat16 [3072, 128], P(('psr', 'toa')), may hold values from -6 to 6
- slot_pulsar: int32 [3072], P(('psr', 'toa')), may hold values from 0 to 7, as said below
- slot_rows: int32 [3072], P(('psr', 'toa')), may hold values from 0 to 128, as said below
- own_prior: float32 [64, 192], P(('psr', 'toa')), may hold values from 0.2 to 5
- spectrum: float32 [32], replicated, may hold values from 0.05 to 2
- directions: float32 [3, 64], replicated, may hold values from -1 to 1, as said below
Outputs:
- coeffs: float32 [64, 64], P(('psr', 'toa'))
- log_dets: float32 [64], P(('psr', 'toa'))
- chi_square: float32 [64], P(('psr', 'toa'))
Inputs may be any that keep to these rules, and one draw needn't show every extreme that they name: `slot_pulsar`: pulsar k of group g is pulsar g * 8 + k of the arrays with a pulsar dimension; empty blocks name pulsar 0. `slot_rows`: on each device the blocks holding TOAs come first and the empty ones (0 rows) last; within a psr group a pulsar's blocks are consecutive in device order, cyclically, all full but its last; every pulsar has between 4 * 96 * 4 and 4 * 96 * 16 TOAs. `directions`: unit vectors; any two are at least 0.1 radians apart.
All inputs are finite; a program needn't handle non-finite values.
Results may differ from a plain program's by a relative error of at most 0.003.
Values sent between devices are 32-bit elements; how exact they have to be, the bound alone decides.
A program may use at most 128 MiB of HBM per device.

v0:
```python
import functools

import jax
import jax.numpy as jnp
from jax import lax
from jax.experimental import pallas as pl
from jax.experimental.pallas import tpu as pltpu
from jax.sharding import PartitionSpec as P

GROUP_PULSARS = 8
ITERS = 8
SIDE = 64
STEP_SLOTS = 8
highest = lax.Precision.HIGHEST


def dot(a, b, precision=highest):
    return jnp.dot(a, b, precision=precision, preferred_element_type=jnp.float32)


def gram_kernel(pulsar_ref, rows_ref, design_ref, weight_ref, residual_ref, out_ref):
    step = pl.program_id(0)
    toas, columns = design_ref.shape[1], design_ref.shape[2]

    @pl.when(step == 0)
    def _():
        out_ref[...] = jnp.zeros_like(out_ref)

    lanes = lax.broadcasted_iota(jnp.int32, (1, toas), 1)
    for j in range(STEP_SLOTS):
        slot = step * STEP_SLOTS + j
        p = pulsar_ref[slot]
        valid = lanes < rows_ref[slot]
        weight = jnp.where(valid, weight_ref[j : j + 1, :], 0.0)
        residual = residual_ref[j : j + 1, :].astype(jnp.float32)
        block = design_ref[j]
        across = jnp.transpose(block).astype(jnp.float32)
        weighted = (across * weight).astype(jnp.bfloat16)
        gram = jnp.dot(weighted, block, preferred_element_type=jnp.float32)
        spread = jnp.broadcast_to(residual, (8, toas)).astype(jnp.bfloat16)
        fitted = lax.dot_general(
            spread, weighted, (((1,), (1,)), ((), ())), preferred_element_type=jnp.float32
        )
        energy = weight * residual * residual
        count = jnp.where(valid, 1.0, 0.0)
        tail = jnp.concatenate([energy, count], axis=1)
        at_row = lax.broadcasted_iota(jnp.int32, (8, columns), 0)
        extra = jnp.where(at_row == 0, fitted, jnp.where(at_row == 1, tail, 0.0))
        out_ref[p, 0:columns, :] += gram
        out_ref[p, columns : columns + 8, :] += extra


def local_grams(design, noise_weight, residuals, slot_pulsar, slot_rows):
    slots, toas, columns = design.shape
    return pl.pallas_call(
        gram_kernel,
        grid_spec=pltpu.PrefetchScalarGridSpec(
            num_scalar_prefetch=2,
            grid=(slots // STEP_SLOTS,),
            in_specs=[
                pl.BlockSpec((STEP_SLOTS, toas, columns), lambda i, *_: (i, 0, 0)),
                pl.BlockSpec((STEP_SLOTS, toas), lambda i, *_: (i, 0)),
                pl.BlockSpec((STEP_SLOTS, toas), lambda i, *_: (i, 0)),
            ],
            out_specs=pl.BlockSpec((GROUP_PULSARS, columns + 8, columns), lambda i, *_: (0, 0, 0)),
        ),
        out_shape=jax.ShapeDtypeStruct((GROUP_PULSARS, columns + 8, columns), jnp.float32),
        name="gram",
    )(slot_pulsar, slot_rows, design, noise_weight, residuals)


def invert(mats):
    side = mats[0].shape[0]
    lane = lax.broadcasted_iota(jnp.int32, (1, side), 1)
    sub = lax.broadcasted_iota(jnp.int32, (side, side), 0)
    lane_full = lax.broadcasted_iota(jnp.int32, (side, side), 1)
    pivots = [jnp.ones((1, side), jnp.float32) for _ in mats]
    mats = list(mats)
    for k in range(side):
        for m, a in enumerate(mats):
            row = a[k : k + 1, :]
            col = a[:, k : k + 1]
            pivot = a[k : k + 1, k : k + 1]
            inverse = 1.0 / pivot
            pivots[m] = jnp.where(lane == k, pivot, pivots[m])
            row = jnp.where(lane == k, 1.0, row) * inverse
            kept = jnp.where(lane_full == k, 0.0, a)
            mats[m] = jnp.where(sub == k, row, kept - col * row)
    return mats, [jnp.sum(jnp.log(v), axis=1, keepdims=True) for v in pivots]


def coupling_kernel(directions_ref, out_ref):
    d = directions_ref[...]
    cosines = jnp.clip(
        lax.dot_general(d, d, (((0,), (0,)), ((), ())), precision=highest, preferred_element_type=jnp.float32),
        -1.0,
        1.0,
    )
    number = cosines.shape[0]
    row = lax.broadcasted_iota(jnp.int32, (number, number), 0)
    col = lax.broadcasted_iota(jnp.int32, (number, number), 1)
    spread = jnp.where(row == col, 1.0, 0.5 * (1.0 - cosines))
    curve = 1.5 * spread * jnp.log(spread) - 0.25 * spread + 0.5
    x = jnp.where(row == col, 1.0, curve)
    side = min(SIDE, number)
    for b in range(number // side):
        lo, hi = b * side, (b + 1) * side
        (inverse,), _ = invert([x[lo:hi, lo:hi]])
        if number == side:
            x = inverse
            continue
        across = dot(inverse, x[lo:hi, :])
        down = x[:, lo:hi]
        inside_row = (row >= lo) & (row < hi)
        inside_col = (col >= lo) & (col < hi)
        updated = x - dot(down, across)
        placed = -dot(down, inverse)
        tiles = number // side
        updated = jnp.where(inside_col, jnp.concatenate([placed] * tiles, axis=1), updated)
        fixed = jnp.where(inside_col, jnp.concatenate([jnp.concatenate([inverse] * tiles, axis=1)] * tiles, axis=0),
                          jnp.concatenate([across] * tiles, axis=0))
        x = jnp.where(inside_row, fixed, updated)
    out_ref[...] = x


def coupling_inverse(directions):
    number = directions.shape[1]
    padded = jnp.pad(directions, ((0, 8 - directions.shape[0]), (0, 0)))
    return pl.pallas_call(
        coupling_kernel,
        out_shape=jax.ShapeDtypeStruct((number, number), jnp.float32),
        cost_estimate=pl.CostEstimate(flops=number**3 * 60, bytes_accessed=4 * number * number, transcendentals=0),
        name="coupling",
    )(padded)


def eliminate_kernel(toa_devices, sums_ref, prior_ref, coupling_ref, power_ref, packed_ref, extra_ref, work_ref):
    owned, height, columns = sums_ref.shape
    common = columns - prior_ref.shape[2]
    device = lax.axis_index("psr") * toa_devices + lax.axis_index("toa")
    row = lax.broadcasted_iota(jnp.int32, (height, columns), 0)
    col = lax.broadcasted_iota(jnp.int32, (height, columns), 1)
    energies, counts = [], []
    for i in range(owned):
        diag = jnp.concatenate([jnp.zeros((1, common), jnp.float32), 1.0 / prior_ref[i]], axis=1)
        tail = sums_ref[i, columns + 1 : columns + 2, :]
        energies.append(jnp.sum(tail[:, : columns // 2], axis=1, keepdims=True))
        counts.append(jnp.sum(tail[:, columns // 2 :], axis=1, keepdims=True))
        work_ref[i] = sums_ref[i] + jnp.where(row == col, diag, 0.0)
    logs = [jnp.zeros((1, 1), jnp.float32)] * owned
    quads = [jnp.zeros((1, 1), jnp.float32)] * owned
    for lo in range(common, columns, SIDE):
        hi = lo + SIDE
        inverses, extra_logs = invert([work_ref[i, lo:hi, lo:hi] for i in range(owned)])
        for i in range(owned):
            logs[i] = logs[i] + extra_logs[i]
            down = work_ref[i, :, lo:hi]
            scaled = dot(down, inverses[i])
            quads[i] = quads[i] + jnp.sum(
                scaled[columns : columns + 1] * down[columns : columns + 1], axis=1, keepdims=True
            )
            work_ref[i] = work_ref[i] - dot(scaled, work_ref[i, lo:hi, :])
    lane_p = lax.broadcasted_iota(jnp.int32, (1, coupling_ref.shape[1]), 1)
    rc = lax.broadcasted_iota(jnp.int32, (common, common), 0)
    cc = lax.broadcasted_iota(jnp.int32, (common, common), 1)
    blocks = []
    for i in range(owned):
        p = device * owned + i
        own = jnp.sum(jnp.where(lane_p == p, coupling_ref[pl.ds(p, 1), :], 0.0), axis=1, keepdims=True)
        blocks.append(work_ref[i, :common, :common] + jnp.where(rc == cc, own * power_ref[...], 0.0))
    inverses, block_logs = invert(blocks)
    half = common // 2
    lane = lax.broadcasted_iota(jnp.int32, (1, 128 - common), 1)
    for i in range(owned):
        packed_ref[i, 0:half, :] = jnp.concatenate([inverses[i][:half], inverses[i][half:]], axis=1)
        target = work_ref[i, columns : columns + 1, :common]
        facts = jnp.where(lane == 0, (logs[i] + block_logs[i]) / columns, 0.0)
        facts = jnp.where(lane == 1, energies[i] - quads[i], facts)
        facts = jnp.where(lane == 2, counts[i], facts)
        line = jnp.concatenate([target, facts], axis=1)
        packed_ref[i, half : half + 8, :] = jnp.broadcast_to(line, (8, 128))
        extra_ref[i : i + 1, :] = line


def eliminate(sums, own_prior, coupling, power, toa_devices):
    owned, height, columns = sums.shape
    common = columns - own_prior.shape[1]
    return pl.pallas_call(
        functools.partial(eliminate_kernel, toa_devices),
        out_shape=(
            jax.ShapeDtypeStruct((owned, common // 2 + 8, 2 * common), jnp.float32),
            jax.ShapeDtypeStruct((owned, 2 * common), jnp.float32),
        ),
        scratch_shapes=[pltpu.VMEM((owned, height, columns), jnp.float32)],
        name="eliminate",
    )(sums, own_prior[:, None, :], coupling, power)


def conjugate_kernel(packed_ref, coupling_ref, power_ref, out_ref, blocks_ref, w_ref):
    number = coupling_ref.shape[0]
    common = power_ref.shape[0]
    half = common // 2
    stride = half + 8

    def spread(k, carry):
        x = jnp.transpose(packed_ref[pl.ds(k, number, stride=stride), :])
        blocks_ref[k] = x[:common]
        blocks_ref[k + half] = x[common:]
        return carry

    lax.fori_loop(0, half, spread, 0)
    target = jnp.transpose(packed_ref[pl.ds(half, number, stride=stride), :])[:common]
    row = lax.broadcasted_iota(jnp.int32, (number, number), 0)
    col = lax.broadcasted_iota(jnp.int32, (number, number), 1)
    mixing = jnp.where(row == col, 0.0, coupling_ref[...])
    power = power_ref[...]

    def total(x):
        return jnp.sum(jnp.sum(x, axis=0, keepdims=True), axis=1, keepdims=True)

    def apply_blocks(v):
        w_ref[...] = v
        acc = jnp.zeros((common, number), jnp.float32)
        for k in range(common):
            acc = acc + blocks_ref[k] * w_ref[k : k + 1, :]
        return acc

    solution = jnp.zeros((common, number), jnp.float32)
    residual = target
    scaled = apply_blocks(residual)
    direction, block_direction = scaled, residual
    inner = total(residual * scaled)
    for iteration in range(ITERS):
        coupled = power * dot(direction, mixing)
        mapped = block_direction + coupled
        step = inner / total(direction * mapped)
        solution = solution + step * direction
        if iteration + 1 < ITERS:
            residual = residual - step * mapped
            scaled = scaled - step * (direction + apply_blocks(coupled))
            following = total(residual * scaled)
            ratio = following / inner
            direction = scaled + ratio * direction
            block_direction = residual + ratio * block_direction
            inner = following
    out_ref[...] = jnp.transpose(solution)


def conjugate(packed, coupling, power):
    number = coupling.shape[0]
    common = power.shape[0]
    return pl.pallas_call(
        conjugate_kernel,
        out_shape=jax.ShapeDtypeStruct((number, common), jnp.float32),
        scratch_shapes=[
            pltpu.VMEM((common, common, number), jnp.float32),
            pltpu.VMEM((common, number), jnp.float32),
        ],
        name="conjugate",
    )(packed.reshape(-1, packed.shape[-1]), coupling, power)


MESH = pl.DeviceIdType.MESH


def reduce_kernel(chips, partial_ref, out_ref, near_ref, sum_ref, far_ref, near_send, near_recv, far_send, far_recv):
    me = lax.axis_index("toa")
    core = lax.rem(me, 2)
    chip = me // 2
    other = 1 - core
    owned = out_ref.shape[0]
    barrier = pltpu.get_barrier_semaphore()
    pl.semaphore_signal(barrier, inc=1, device_id={"toa": chip * 2 + other}, device_id_type=MESH)
    for d in range(1, chips):
        target = lax.rem(chip + d, chips) * 2 + core
        pl.semaphore_signal(barrier, inc=1, device_id={"toa": target}, device_id_type=MESH)
    pl.semaphore_wait(barrier, chips)
    order = [d % chips for d in range(1, chips + 1)]
    near, far = {}, {}
    for d in order:
        owner = lax.rem(chip + d, chips) * 2 + other
        for i in range(owned):
            near[d, i] = pltpu.make_async_remote_copy(
                src_ref=partial_ref.at[owner * owned + i],
                dst_ref=near_ref.at[d * owned + i],
                send_sem=near_send.at[d * owned + i],
                recv_sem=near_recv.at[d * owned + i],
                device_id={"toa": chip * 2 + other},
                device_id_type=MESH,
            )
            near[d, i].start()
    for d in order:
        owner = lax.rem(chip + d, chips) * 2 + core
        for i in range(owned):
            at = d * owned + i
            near[d, i].wait_recv()
            both = partial_ref[owner * owned + i] + near_ref[at]
            if d == 0:
                out_ref[i] = both
                continue
            sum_ref[at - owned] = both
            far[d, i] = pltpu.make_async_remote_copy(
                src_ref=sum_ref.at[at - owned],
                dst_ref=far_ref.at[at - owned],
                send_sem=far_send.at[at - owned],
                recv_sem=far_recv.at[at - owned],
                device_id={"toa": owner},
                device_id_type=MESH,
            )
            far[d, i].start()
    for (d, i), copy in far.items():
        copy.wait_recv()
        out_ref[i] += far_ref[d * owned + i - owned]
    for copy in list(near.values()) + list(far.values()):
        copy.wait_send()


def reduce_owners(partial, toa_devices):
    pulsars, height, columns = partial.shape
    owned = pulsars // toa_devices
    chips = toa_devices // 2
    moved = owned * (chips - 1)
    block = (height, columns)
    return pl.pallas_call(
        functools.partial(reduce_kernel, chips),
        out_shape=jax.ShapeDtypeStruct((owned,) + block, jnp.float32),
        in_specs=[pl.BlockSpec(memory_space=pltpu.VMEM)],
        out_specs=pl.BlockSpec(memory_space=pltpu.VMEM),
        scratch_shapes=[
            pltpu.VMEM((owned * chips,) + block, jnp.float32),
            pltpu.VMEM((moved,) + block, jnp.float32),
            pltpu.VMEM((moved,) + block, jnp.float32),
            pltpu.SemaphoreType.DMA((owned * chips,)),
            pltpu.SemaphoreType.DMA((owned * chips,)),
            pltpu.SemaphoreType.DMA((moved,)),
            pltpu.SemaphoreType.DMA((moved,)),
        ],
        compiler_params=pltpu.CompilerParams(collective_id=0, has_side_effects=True),
        cost_estimate=pl.CostEstimate(flops=4 * pulsars * height * columns, bytes_accessed=40 * pulsars * height * columns, transcendentals=0),
        name="reduce_owners",
    )(partial)


def gather_kernel(groups, chips, mine_ref, out_ref, all_ref, psr_send, chip_send, core_send, recv):
    psr, me = lax.axis_index("psr"), lax.axis_index("toa")
    toa_devices = 2 * chips
    core = lax.rem(me, 2)
    chip = me // 2
    other = 1 - core
    partner = chip * 2 + other
    barrier = pltpu.get_barrier_semaphore()

    def greet(psr_to, toa_to):
        pl.semaphore_signal(barrier, inc=1, device_id={"psr": psr_to, "toa": toa_to}, device_id_type=MESH)

    greet(psr, partner)
    for d in range(1, chips):
        greet(psr, lax.rem(chip + d, chips) * 2 + core)
    for e in range(1, groups):
        greet(lax.rem(psr + e, groups), me)
    pl.semaphore_wait(barrier, chips + groups - 1)
    sent = []

    def block_of(e, toa):
        return lax.rem(psr + groups - e, groups) * toa_devices + toa

    def copy(source, block, sem, psr_to, toa_to):
        return pltpu.make_async_remote_copy(
            src_ref=source,
            dst_ref=all_ref.at[block],
            send_sem=sem,
            recv_sem=recv.at[block],
            device_id={"psr": psr_to, "toa": toa_to},
            device_id_type=MESH,
        )

    def send(source, block, sem, psr_to, toa_to):
        moving = copy(source, block, sem, psr_to, toa_to)
        moving.start()
        sent.append(moving)

    def arrived(block):
        copy(all_ref.at[block], block, core_send.at[0], psr, partner).wait_recv()

    own = psr * toa_devices + me
    for e in range(1, groups):
        send(mine_ref, own, psr_send.at[e - 1], lax.rem(psr + e, groups), me)
    for e in range(groups):
        block = block_of(e, me)
        if e:
            arrived(block)
        source = all_ref.at[block] if e else mine_ref
        for d in range(1, chips):
            send(source, block, chip_send.at[e * (chips - 1) + d - 1], psr, lax.rem(chip + d, chips) * 2 + core)
        send(source, block, core_send.at[e], psr, partner)
    for d in range(1, chips):
        for e in range(groups):
            block = block_of(e, lax.rem(chip + chips - d, chips) * 2 + core)
            arrived(block)
            send(all_ref.at[block], block, core_send.at[d * groups + e], psr, partner)
    all_ref[own] = mine_ref[...]
    for c in range(chips):
        for e in range(groups):
            arrived(block_of(e, c * 2 + other))
    for moving in sent:
        moving.wait_send()
    out_ref[...] = all_ref[...]


def gather_all(mine, groups, toa_devices):
    chips = toa_devices // 2
    devices = groups * toa_devices
    return pl.pallas_call(
        functools.partial(gather_kernel, groups, chips),
        out_shape=jax.ShapeDtypeStruct((devices,) + mine.shape, jnp.float32),
        in_specs=[pl.BlockSpec(memory_space=pltpu.VMEM)],
        out_specs=pl.BlockSpec(memory_space=pltpu.VMEM),
        scratch_shapes=[
            pltpu.VMEM((devices,) + mine.shape, jnp.float32),
            pltpu.SemaphoreType.DMA((groups - 1,)),
            pltpu.SemaphoreType.DMA((groups * (chips - 1),)),
            pltpu.SemaphoreType.DMA((groups * chips,)),
            pltpu.SemaphoreType.DMA((devices,)),
        ],
        compiler_params=pltpu.CompilerParams(collective_id=1, has_side_effects=True),
        name="gather_all",
    )(mine)


def body(design, noise_weight, residuals, slot_pulsar, slot_rows, own_prior, spectrum, directions):
    toa_devices = lax.axis_size("toa")
    owned = GROUP_PULSARS // toa_devices
    device = lax.axis_index("psr") * toa_devices + lax.axis_index("toa")
    partial = local_grams(design, noise_weight, residuals, slot_pulsar, slot_rows)
    sums = reduce_owners(partial, toa_devices)
    coupling = coupling_inverse(directions)
    power = 1.0 / jnp.repeat(spectrum, 2)
    packed, extra = eliminate(sums, own_prior, coupling, power[None, :], toa_devices)
    mine = packed.reshape(-1, packed.shape[-1])
    everything = gather_all(mine, lax.axis_size("psr"), toa_devices)
    whole = conjugate(everything, coupling, power[:, None])
    common = whole.shape[1]
    solution = lax.dynamic_slice_in_dim(whole, device * owned, owned, 0)
    chi_square = (extra[:, common + 1] - jnp.sum(extra[:, :common] * solution, axis=1)) / extra[:, common + 2]
    return (solution, extra[:, common], chi_square)


def solution(mesh):
    return jax.shard_map(
        body,
        mesh=mesh,
        in_specs=(
            P(("psr", "toa"), None, None),
            P(("psr", "toa"), None),
            P(("psr", "toa"), None),
            P(("psr", "toa")),
            P(("psr", "toa")),
            P(("psr", "toa"), None),
            P(),
            P(),
        ),
        out_specs=(P(("psr", "toa"), None), P(("psr", "toa")), P(("psr", "toa"))),
        check_vma=False,
    )
```

profile of v0, /device:TPU:0, one launch (start us, length us, event | category | flops | bytes accessed | tf_op | source)
XLA Modules:
  0.0 101.5 jit_solution(1325230494462956786)
XLA Ops:
  0.6 12.9 %gram.1.partial_ref = f32[8,264,256]{2,1,0:T(8,128)} custom-call(s32[96]{0:T(128)} %pulsar_ref.1, s32[96]{0:T(128)} %rows_ref.1, bf16[96,128,256]{2,1,0:T(8,128)(2,1)} %design_ref.1, f32[96,128]{1,0:T(8,128)} %weight_ref.1, bf16[96,128]{1,0:T(8,128)(2,1)} %residual_ref.1), custom_call_target="tpu_custom_call" | custom-call | tf_op jit(solution)/shard_map/gram/pallas_call | solution.py:55
  13.5 0.0 copy-start.1
  13.5 0.0 copy-start.2
  13.5 0.0 copy-start.3
  13.5 19.6 %reduce_owners.1.sums_ref = f32[2,264,256]{2,1,0:T(8,128)} custom-call(f32[8,264,256]{2,1,0:T(8,128)} %gram.1.partial_ref), custom_call_target="tpu_custom_call" | custom-call | flops 2162688 | bytes 21626880 | tf_op jit(solution)/shard_map/reduce_owners/pallas_call | solution.py:324
  33.1 0.0 copy-done.1
  33.1 0.6 broadcast_in_dim.8.prior_ref
  33.7 0.0 copy-done.2
  33.7 0.6 pad.4.directions_ref
  34.3 6.9 %coupling.1.coupling_ref = f32[64,64]{1,0:T(8,128)} custom-call(f32[8,64]{1,0:T(8,128)} %pad.4.directions_ref), custom_call_target="tpu_custom_call" | custom-call | flops 15728640 | bytes 16384 | tf_op jit(solution)/shard_map/coupling/pallas_call | solution.py:129
  41.3 0.0 copy-done.3
  41.3 0.1 broadcast_in_dim.9
  41.4 0.6 div.33.power_ref
  42.0 27.8 %eliminate.1 = (f32[2,40,128]{2,1,0:T(8,128)}, f32[2,128]{1,0:T(2,128)}) custom-call(f32[2,264,256]{2,1,0:T(8,128)} %reduce_owners.1.sums_ref, f32[2,1,192]{2,1,0:T(1,128)} %broadcast_in_dim.8.prior_ref, f32[64,64]{1,0:T(8,128)} %coupling.1.coupling_ref, f32[1,64]{1,0:T(1,128)} %div.33.power_ref), custom_call_target="tpu_custom_call" | custom-call | tf_op jit(solution)/shard_map/eliminate/pallas_call | solution.py:188
  69.8 0.0 copy-start
  69.8 19.8 %gather_all.1 = f32[32,80,128]{2,1,0:T(8,128)} custom-call(f32[80,128]{1,0:T(8,128)} %bitcast.3), custom_call_target="tpu_custom_call" | custom-call | tf_op jit(solution)/shard_map/gather_all/pallas_call | solution.py:413
  89.5 0.7 div.36.power_ref
  90.2 8.7 %conjugate.1 = f32[64,64]{1,0:T(8,128)} custom-call(f32[2560,128]{1,0:T(8,128)} %bitcast.2, f32[64,64]{1,0:T(8,128)} %coupling.1.coupling_ref, f32[64,1]{1,0:T(8,128)} %div.36.power_ref), custom_call_target="tpu_custom_call" | custom-call | tf_op jit(solution)/shard_map/conjugate/pallas_call | solution.py:252
  98.9 0.0 copy-done
  98.9 1.4 %multiply_reduce_fusion = (f32[2]{0:T(128)S(1)}, f32[2,64]{1,0:T(2,128)}) fusion(f32[2,128]{1,0:T(2,128)S(1)} %copy-done, f32[64,64]{1,0:T(8,128)} %conjugate.1, s32[]{:T(128)S(6)} %select_n.3), kind=kLoop, calls=%fused_computation.1 | loop fusion | flops 254 | bytes 1548 | tf_op jit(solution)/shard_map/reduce_sum | solution.py:444
  100.2 0.7 slice_reduce_fusion.1
  100.9 0.5 subtract_divide_fusion
  (1 shorter events, 0.0 us)
Async XLA Ops:
  13.5 19.6 %copy-start.1 = (f32[2,192]{1,0:T(2,128)S(1)}, f32[2,192]{1,0:T(2,128)}, u32[]{:S(2)}) copy-start(f32[2,192]{1,0:T(2,128)} %param.13) | copy-start | bytes 4612
  13.5 20.2 %copy-start.2 = (f32[3,64]{1,0:T(4,128)S(1)}, f32[3,64]{1,0:T(4,128)}, u32[]{:S(2)}) copy-start(f32[3,64]{1,0:T(4,128)} %param.15) | copy-start | bytes 2308
  13.5 27.8 %copy-start.3 = (f32[32]{0:T(128)S(1)}, f32[32]{0:T(128)}, u32[]{:S(2)}) copy-start(f32[32]{0:T(128)} %param.14) | copy-start | bytes 388
  69.8 29.1 %copy-start = (f32[2,128]{1,0:T(2,128)S(1)}, f32[2,128]{1,0:T(2,128)}, u32[]{:S(2)}) copy-start(f32[2,128]{1,0:T(2,128)} %get-tuple-element.6) | copy-start | bytes 3076
where the time goes:
time: 102 us; the launch traced here: 101 us
  Pallas kernels  95.6 us (94%)
  local copies, waits for them, and re-layouts  3.27 us (3%)
  other arithmetic  1.88 us (2%)
    pallas_call x1, Pallas kernels, eliminate(): pl.pallas_call(functools.partial(eliminate_kernel, toa_devices), out_shap...  27.8 us
    pallas_call x1, Pallas kernels, gather_all(): pl.pallas_call(functools.partial(gather_kernel, groups, chips), out_shape...  19.8 us
    pallas_call x1, Pallas kernels, reduce_owners(): pl.pallas_call(functools.partial(reduce_kernel, chips), out_shape=jax.Sha...  19.6 us
    pallas_call x1, Pallas kernels, local_grams(): pl.pallas_call(gram_kernel, grid_spec=pltpu.PrefetchScalarGridSpec(num_sc...  12.9 us
    pallas_call x1, Pallas kernels, conjugate(): pl.pallas_call(conjugate_kernel, out_shape=jax.ShapeDtypeStruct((number,...  8.66 us
    pallas_call x1, Pallas kernels, coupling_inverse(): pl.pallas_call(coupling_kernel, out_shape=jax.ShapeDtypeStruct((number, n...  6.95 us

commit v1 on v0

--- a/solution.py
+++ b/solution.py
@@ -11,6 +11,7 @@
 ITERS = 8
 SIDE = 64
 STEP_SLOTS = 8
+PANEL = 16
 highest = lax.Precision.HIGHEST
 
 
@@ -134,52 +135,129 @@
     )(padded)
 
 
-def eliminate_kernel(toa_devices, sums_ref, prior_ref, coupling_ref, power_ref, packed_ref, extra_ref, work_ref):
+def invert_pair(x, width):
+    side, lanes = x.shape
+    lane = lax.broadcasted_iota(jnp.int32, (1, lanes), 1)
+    within = lax.rem(lane, side)
+    half = lax.broadcasted_iota(jnp.int32, (side, lanes), 1)
+    half = half - lax.rem(half, side)
+    pivots = jnp.ones((1, lanes), jnp.float32)
+    for lo in range(0, side, width):
+        hi = lo + width
+        columns = [jnp.take_along_axis(x, half + (lo + k), axis=1) for k in range(width)]
+        rows = x[lo:hi]
+        inner = [c[lo:hi] for c in columns]
+        sub = lax.broadcasted_iota(jnp.int32, (width, lanes), 0)
+        for k in range(width):
+            here = within == lo + k
+            pivot = inner[k][k : k + 1]
+            inverse = 1.0 / pivot
+            pivots = jnp.where(here, pivot, pivots)
+            row = jnp.where(here, 1.0, rows[k : k + 1]) * inverse
+            at = sub == k
+            rows = jnp.where(at, row, jnp.where(here, 0.0, rows) - inner[k] * row)
+            for j in range(k + 1, width):
+                scaled = inner[j][k : k + 1] * inverse
+                inner[j] = jnp.where(at, scaled, inner[j] - inner[k] * scaled)
+        inside = (within >= lo) & (within < hi)
+        parts = []
+        for begin in range(0, side, width):
+            if begin == lo:
+                parts.append(rows)
+                continue
+            acc = jnp.where(inside, 0.0, x[begin : begin + width])
+            for k in range(width):
+                acc = acc - columns[k][begin : begin + width] * rows[k : k + 1]
+            parts.append(acc)
+        x = jnp.concatenate(parts, axis=0)
+    return x, jnp.log(pivots)
+
+
+def paired(block):
+    side, lanes = block.shape
+    lane = lax.broadcasted_iota(jnp.int32, (side, lanes), 1)
+    return jnp.concatenate([jnp.where(lane < side, block, 0.0), jnp.where(lane >= side, block, 0.0)], axis=0)
+
+
+def dot_paired(a, block):
+    return dot(a, paired(block))
+
+
+def dot_paired_t(a, block):
+    return lax.dot_general(
+        a, paired(block), (((1,), (1,)), ((), ())), precision=highest, preferred_element_type=jnp.float32
+    )
+
+
+def halves(row, side):
+    lane = lax.broadcasted_iota(jnp.int32, row.shape, 1)
+    return [
+        jnp.sum(jnp.where(lane < side, row, 0.0), axis=1, keepdims=True),
+        jnp.sum(jnp.where(lane >= side, row, 0.0), axis=1, keepdims=True),
+    ]
+
+
+def eliminate_kernel(toa_devices, sums_ref, prior_ref, coupling_ref, power_ref, packed_ref, extra_ref):
     owned, height, columns = sums_ref.shape
+    side = SIDE
     common = columns - prior_ref.shape[2]
     device = lax.axis_index("psr") * toa_devices + lax.axis_index("toa")
-    row = lax.broadcasted_iota(jnp.int32, (height, columns), 0)
-    col = lax.broadcasted_iota(jnp.int32, (height, columns), 1)
-    energies, counts = [], []
-    for i in range(owned):
-        diag = jnp.concatenate([jnp.zeros((1, common), jnp.float32), 1.0 / prior_ref[i]], axis=1)
-        tail = sums_ref[i, columns + 1 : columns + 2, :]
-        energies.append(jnp.sum(tail[:, : columns // 2], axis=1, keepdims=True))
-        counts.append(jnp.sum(tail[:, columns // 2 :], axis=1, keepdims=True))
-        work_ref[i] = sums_ref[i] + jnp.where(row == col, diag, 0.0)
-    logs = [jnp.zeros((1, 1), jnp.float32)] * owned
-    quads = [jnp.zeros((1, 1), jnp.float32)] * owned
-    for lo in range(common, columns, SIDE):
-        hi = lo + SIDE
-        inverses, extra_logs = invert([work_ref[i, lo:hi, lo:hi] for i in range(owned)])
-        for i in range(owned):
-            logs[i] = logs[i] + extra_logs[i]
-            down = work_ref[i, :, lo:hi]
-            scaled = dot(down, inverses[i])
-            quads[i] = quads[i] + jnp.sum(
-                scaled[columns : columns + 1] * down[columns : columns + 1], axis=1, keepdims=True
-            )
-            work_ref[i] = work_ref[i] - dot(scaled, work_ref[i, lo:hi, :])
     lane_p = lax.broadcasted_iota(jnp.int32, (1, coupling_ref.shape[1]), 1)
-    rc = lax.broadcasted_iota(jnp.int32, (common, common), 0)
-    cc = lax.broadcasted_iota(jnp.int32, (common, common), 1)
-    blocks = []
-    for i in range(owned):
-        p = device * owned + i
-        own = jnp.sum(jnp.where(lane_p == p, coupling_ref[pl.ds(p, 1), :], 0.0), axis=1, keepdims=True)
-        blocks.append(work_ref[i, :common, :common] + jnp.where(rc == cc, own * power_ref[...], 0.0))
-    inverses, block_logs = invert(blocks)
-    half = common // 2
-    lane = lax.broadcasted_iota(jnp.int32, (1, 128 - common), 1)
-    for i in range(owned):
-        packed_ref[i, 0:half, :] = jnp.concatenate([inverses[i][:half], inverses[i][half:]], axis=1)
-        target = work_ref[i, columns : columns + 1, :common]
-        facts = jnp.where(lane == 0, (logs[i] + block_logs[i]) / columns, 0.0)
-        facts = jnp.where(lane == 1, energies[i] - quads[i], facts)
-        facts = jnp.where(lane == 2, counts[i], facts)
-        line = jnp.concatenate([target, facts], axis=1)
-        packed_ref[i, half : half + 8, :] = jnp.broadcast_to(line, (8, 128))
-        extra_ref[i : i + 1, :] = line
+    lane2 = lax.broadcasted_iota(jnp.int32, (1, 2 * side), 1)
+    row2 = lax.broadcasted_iota(jnp.int32, (side, 2 * side), 0)
+    col2 = lax.rem(lax.broadcasted_iota(jnp.int32, (side, 2 * side), 1), side)
+    blocks = columns // side
+    power = power_ref[...]
+    power2 = jnp.concatenate([power, power], axis=1)
+    for first in range(0, owned, 2):
+        pair = (first, min(first + 1, owned - 1))
+
+        def both(lo, hi, j):
+            return jnp.concatenate([sums_ref[p, lo:hi, j * side : (j + 1) * side] for p in pair], axis=1)
+
+        order = list(range(1, blocks)) + [0]
+        a = {}
+        for s, j in enumerate(order):
+            for i in order[s:]:
+                a[i, j] = both(i * side, (i + 1) * side, j)
+            a["p", j] = both(columns, columns + 8, j)
+            if j:
+                own = jnp.concatenate([1.0 / prior_ref[p, :, (j - 1) * side : j * side] for p in pair], axis=1)
+                a[j, j] = a[j, j] + jnp.where(row2 == col2, own, 0.0)
+        logs = jnp.zeros((1, 2 * side), jnp.float32)
+        quads = jnp.zeros((1, 2 * side), jnp.float32)
+        for s, j in enumerate(order[:-1]):
+            inverse, extra_logs = invert_pair(a[j, j], PANEL)
+            logs = logs + extra_logs
+            rest = order[s + 1 :]
+            scaled = {i: dot_paired(a[i, j], inverse) for i in rest + ["p"]}
+            quads = quads + scaled["p"][0:1] * a["p", j][0:1]
+            for t, m in enumerate(rest):
+                for i in rest[t:] + ["p"]:
+                    a[i, m] = a[i, m] - dot_paired_t(scaled[i], a[m, j])
+        owns = []
+        for p in pair:
+            at = device * owned + p
+            owns.append(jnp.sum(jnp.where(lane_p == at, coupling_ref[pl.ds(at, 1), :], 0.0), axis=1, keepdims=True))
+        own2 = jnp.where(lane2 < side, owns[0], owns[1])
+        inverse, extra_logs = invert_pair(a[0, 0] + jnp.where(row2 == col2, own2 * power2, 0.0), PANEL)
+        logs = halves(logs + extra_logs, side)
+        quads = halves(quads, side)
+        lane = lax.broadcasted_iota(jnp.int32, (1, 128 - common), 1)
+        half = common // 2
+        for h, p in enumerate(pair[: min(2, owned - first)]):
+            tail = sums_ref[p, columns + 1 : columns + 2, :]
+            energy = jnp.sum(tail[:, : columns // 2], axis=1, keepdims=True)
+            count = jnp.sum(tail[:, columns // 2 :], axis=1, keepdims=True)
+            mine = inverse[:, h * side : (h + 1) * side]
+            packed_ref[p, 0:half, :] = jnp.concatenate([mine[:half], mine[half:]], axis=1)
+            target = a["p", 0][0:1, h * side : (h + 1) * side]
+            facts = jnp.where(lane == 0, logs[h] / columns, 0.0)
+            facts = jnp.where(lane == 1, energy - quads[h], facts)
+            facts = jnp.where(lane == 2, count, facts)
+            line = jnp.concatenate([target, facts], axis=1)
+            packed_ref[p, half : half + 8, :] = jnp.broadcast_to(line, (8, 128))
+            extra_ref[p : p + 1, :] = line
 
 
 def eliminate(sums, own_prior, coupling, power, toa_devices):
@@ -191,7 +269,6 @@
             jax.ShapeDtypeStruct((owned, common // 2 + 8, 2 * common), jnp.float32),
             jax.ShapeDtypeStruct((owned, 2 * common), jnp.float32),
         ),
-        scratch_shapes=[pltpu.VMEM((owned, height, columns), jnp.float32)],
         name="eliminate",
     )(sums, own_prior[:, None, :], coupling, power)
 

time: 102 us -> 84.4 us (0.83)
  Pallas kernels: 95.6 us -> 78 us
    pallas_call x1, Pallas kernels: 27.8 us -> 10.2 us  [eliminate(): pl.pallas_call(functools.partial(eliminate_kernel, toa_devices), out_shap...]
where the time goes in v1:
time: 84.4 us; the launch traced here: 83.9 us
  Pallas kernels  78 us (92%)
  local copies, waits for them, and re-layouts  3.27 us (4%)
  other arithmetic  1.88 us (2%)
    pallas_call x1, Pallas kernels, gather_all(): pl.pallas_call(functools.partial(gather_kernel, groups, chips), out_shape...  19.8 us
    pallas_call x1, Pallas kernels, reduce_owners(): pl.pallas_call(functools.partial(reduce_kernel, chips), out_shape=jax.Sha...  19.6 us
    pallas_call x1, Pallas kernels, local_grams(): pl.pallas_call(gram_kernel, grid_spec=pltpu.PrefetchScalarGridSpec(num_sc...  12.9 us
    pallas_call x1, Pallas kernels, eliminate(): pl.pallas_call(functools.partial(eliminate_kernel, toa_devices), out_shap...  10.2 us
    pallas_call x1, Pallas kernels, conjugate(): pl.pallas_call(conjugate_kernel, out_shape=jax.ShapeDtypeStruct((number,...  8.67 us
    pallas_call x1, Pallas kernels, coupling_inverse(): pl.pallas_call(coupling_kernel, out_shape=jax.ShapeDtypeStruct((number, n...  6.95 us

profile of v1, /device:TPU:0, one launch (start us, length us, event | category | flops | bytes accessed | tf_op | source)
XLA Modules:
  0.0 83.9 jit_solution(8645441911447334821)
XLA Ops:
  0.6 12.9 %gram.1.partial_ref = f32[8,264,256]{2,1,0:T(8,128)} custom-call(s32[96]{0:T(128)} %pulsar_ref.1, s32[96]{0:T(128)} %rows_ref.1, bf16[96,128,256]{2,1,0:T(8,128)(2,1)} %design_ref.1, f32[96,128]{1,0:T(8,128)} %weight_ref.1, bf16[96,128]{1,0:T(8,128)(2,1)} %residual_ref.1), custom_call_target="tpu_custom_call" | custom-call | tf_op jit(solution)/shard_map/gram/pallas_call | solution.py:56
  13.5 0.0 copy-start.1
  13.5 0.0 copy-start.2
  13.5 0.0 copy-start.3
  13.5 19.6 %reduce_owners.1.sums_ref = f32[2,264,256]{2,1,0:T(8,128)} custom-call(f32[8,264,256]{2,1,0:T(8,128)} %gram.1.partial_ref), custom_call_target="tpu_custom_call" | custom-call | flops 2162688 | bytes 21626880 | tf_op jit(solution)/shard_map/reduce_owners/pallas_call | solution.py:401
  33.1 0.0 copy-done.1
  33.1 0.6 broadcast_in_dim.8.prior_ref
  33.7 0.0 copy-done.2
  33.7 0.6 pad.4.directions_ref
  34.3 6.9 %coupling.1.coupling_ref = f32[64,64]{1,0:T(8,128)} custom-call(f32[8,64]{1,0:T(8,128)} %pad.4.directions_ref), custom_call_target="tpu_custom_call" | custom-call | flops 15728640 | bytes 16384 | tf_op jit(solution)/shard_map/coupling/pallas_call | solution.py:130
  41.3 0.0 copy-done.3
  41.3 0.1 broadcast_in_dim.9
  41.4 0.6 div.33.power_ref
  42.0 10.2 %eliminate.1 = (f32[2,40,128]{2,1,0:T(8,128)}, f32[2,128]{1,0:T(2,128)}) custom-call(f32[2,264,256]{2,1,0:T(8,128)} %reduce_owners.1.sums_ref, f32[2,1,192]{2,1,0:T(1,128)} %broadcast_in_dim.8.prior_ref, f32[64,64]{1,0:T(8,128)} %coupling.1.coupling_ref, f32[1,64]{1,0:T(1,128)} %div.33.power_ref), custom_call_target="tpu_custom_call" | custom-call | tf_op jit(solution)/shard_map/eliminate/pallas_call | solution.py:266
  52.2 0.0 copy-start
  52.2 19.8 %gather_all.1 = f32[32,80,128]{2,1,0:T(8,128)} custom-call(f32[80,128]{1,0:T(8,128)} %bitcast.3), custom_call_target="tpu_custom_call" | custom-call | tf_op jit(solution)/shard_map/gather_all/pallas_call | solution.py:490
  72.0 0.7 div.36.power_ref
  72.6 8.7 %conjugate.1 = f32[64,64]{1,0:T(8,128)} custom-call(f32[2560,128]{1,0:T(8,128)} %bitcast.2, f32[64,64]{1,0:T(8,128)} %coupling.1.coupling_ref, f32[64,1]{1,0:T(8,128)} %div.36.power_ref), custom_call_target="tpu_custom_call" | custom-call | tf_op jit(solution)/shard_map/conjugate/pallas_call | solution.py:329
  81.3 0.0 copy-done
  81.3 1.4 %multiply_reduce_fusion = (f32[2]{0:T(128)S(1)}, f32[2,64]{1,0:T(2,128)}) fusion(f32[2,128]{1,0:T(2,128)S(1)} %copy-done, f32[64,64]{1,0:T(8,128)} %conjugate.1, s32[]{:T(128)S(6)} %select_n.3), kind=kLoop, calls=%fused_computation.1 | loop fusion | flops 254 | bytes 1548 | tf_op jit(solution)/shard_map/reduce_sum | solution.py:521
  82.7 0.7 slice_reduce_fusion.1
  83.3 0.5 subtract_divide_fusion
  (1 shorter events, 0.0 us)
Async XLA Ops:
  13.5 19.6 %copy-start.1 = (f32[2,192]{1,0:T(2,128)S(1)}, f32[2,192]{1,0:T(2,128)}, u32[]{:S(2)}) copy-start(f32[2,192]{1,0:T(2,128)} %param.13) | copy-start | bytes 4612
  13.5 20.2 %copy-start.2 = (f32[3,64]{1,0:T(4,128)S(1)}, f32[3,64]{1,0:T(4,128)}, u32[]{:S(2)}) copy-start(f32[3,64]{1,0:T(4,128)} %param.15) | copy-start | bytes 2308
  13.5 27.8 %copy-start.3 = (f32[32]{0:T(128)S(1)}, f32[32]{0:T(128)}, u32[]{:S(2)}) copy-start(f32[32]{0:T(128)} %param.14) | copy-start | bytes 388
  52.2 29.1 %copy-start = (f32[2,128]{1,0:T(2,128)S(1)}, f32[2,128]{1,0:T(2,128)}, u32[]{:S(2)}) copy-start(f32[2,128]{1,0:T(2,128)} %get-tuple-element.6) | copy-start | bytes 3076

commit v2 on v0

v2 whole, which is shorter than its diff:
```python
import functools

import jax
import jax.numpy as jnp
from jax import lax
from jax.experimental import pallas as pl
from jax.experimental.pallas import tpu as pltpu
from jax.sharding import PartitionSpec as P

GROUP_PULSARS = 8
ITERS = 8
SIDE = 64
HALF = 32
LANES = 128
STEP_SLOTS = 16
PANEL = 16
highest = lax.Precision.HIGHEST
MESH = pl.DeviceIdType.MESH


def dot(a, b, precision=highest):
    return jnp.dot(a, b, precision=precision, preferred_element_type=jnp.float32)


def iota(shape, axis):
    return lax.broadcasted_iota(jnp.int32, shape, axis)


def gram_kernel(pulsar_ref, rows_ref, design_ref, weight_ref, residual_ref, out_ref, acc_ref):
    step = pl.program_id(0)
    toas, columns = design_ref.shape[1], design_ref.shape[2]
    half = columns // 2

    @pl.when(step == 0)
    def _():
        acc_ref[...] = jnp.zeros_like(acc_ref)

    lanes = iota((1, toas), 1)
    at_row = iota((8, half), 0)
    for j in range(STEP_SLOTS):
        slot = step * STEP_SLOTS + j
        p = pulsar_ref[slot]
        valid = lanes < rows_ref[slot]
        weight = jnp.where(valid, weight_ref[j : j + 1, :], 0.0)
        residual = residual_ref[j : j + 1, :].astype(jnp.float32)
        block = design_ref[j]
        across = jnp.transpose(block).astype(jnp.float32)
        weighted = (across * weight).astype(jnp.bfloat16)
        gram = jnp.dot(weighted, block, preferred_element_type=jnp.float32)
        spread = jnp.broadcast_to(residual, (8, toas)).astype(jnp.bfloat16)
        fitted = lax.dot_general(
            spread, weighted, (((1,), (1,)), ((), ())), preferred_element_type=jnp.float32
        )
        energy = weight * residual * residual
        count = jnp.where(valid, 1.0, 0.0)
        extra = jnp.where(at_row == 0, fitted[:, :half], jnp.where(at_row == 1, fitted[:, half:], 0.0))
        extra = jnp.where(at_row == 2, energy, jnp.where(at_row == 3, count, extra))
        acc_ref[p, 0:half, :] += gram[:half, :half]
        acc_ref[p, half:columns, :] += gram[:half, half:]
        acc_ref[p, columns : columns + half, :] += gram[half:, half:]
        acc_ref[p, columns + half : columns + half + 8, :] += extra

    @pl.when(step == pl.num_programs(0) - 1)
    def _():
        row, col = iota((half, half), 0), iota((half, half), 1)

        def pack(p, carry):
            low = acc_ref[p, columns : columns + half, :]
            out_ref[p, 0:half, :] = jnp.where(row >= col, acc_ref[p, 0:half, :], low)
            out_ref[p, half:columns, :] = acc_ref[p, half:columns, :]
            diag = jnp.sum(jnp.where(row == col, low, 0.0), axis=0, keepdims=True)
            tail = acc_ref[p, columns + half : columns + half + 8, :]
            out_ref[p, columns : columns + 8, :] = jnp.where(at_row == 4, diag, tail)
            return carry

        lax.fori_loop(0, GROUP_PULSARS, pack, 0)


def local_grams(design, noise_weight, residuals, slot_pulsar, slot_rows):
    slots, toas, columns = design.shape
    half = columns // 2
    return pl.pallas_call(
        gram_kernel,
        grid_spec=pltpu.PrefetchScalarGridSpec(
            num_scalar_prefetch=2,
            grid=(slots // STEP_SLOTS,),
            in_specs=[
                pl.BlockSpec((STEP_SLOTS, toas, columns), lambda i, *_: (i, 0, 0)),
                pl.BlockSpec((STEP_SLOTS, toas), lambda i, *_: (i, 0)),
                pl.BlockSpec((STEP_SLOTS, toas), lambda i, *_: (i, 0)),
            ],
            out_specs=pl.BlockSpec((GROUP_PULSARS, columns + 8, half), lambda i, *_: (0, 0, 0)),
            scratch_shapes=[pltpu.VMEM((GROUP_PULSARS, columns + half + 8, half), jnp.float32)],
        ),
        out_shape=jax.ShapeDtypeStruct((GROUP_PULSARS, columns + 8, half), jnp.float32),
        name="gram",
    )(slot_pulsar, slot_rows, design, noise_weight, residuals)


def invert_pair(x, width):
    side, lanes = x.shape
    within = lax.rem(iota((1, lanes), 1), side)
    half = iota((side, lanes), 1)
    half = half - lax.rem(half, side)
    sub = iota((width, lanes), 0)
    pivots = jnp.ones((1, lanes), jnp.float32)
    for lo in range(0, side, width):
        hi = lo + width
        columns = [jnp.take_along_axis(x, half + (lo + k), axis=1) for k in range(width)]
        rows = x[lo:hi]
        inner = [c[lo:hi] for c in columns]
        for k in range(width):
            here = within == lo + k
            pivot = inner[k][k : k + 1]
            inverse = 1.0 / pivot
            pivots = jnp.where(here, pivot, pivots)
            row = jnp.where(here, 1.0, rows[k : k + 1]) * inverse
            at = sub == k
            rows = jnp.where(at, row, jnp.where(here, 0.0, rows) - inner[k] * row)
            for j in range(k + 1, width):
                scaled = inner[j][k : k + 1] * inverse
                inner[j] = jnp.where(at, scaled, inner[j] - inner[k] * scaled)
        inside = (within >= lo) & (within < hi)
        parts = []
        for begin in range(0, side, width):
            if begin == lo:
                parts.append(rows)
                continue
            acc = jnp.where(inside, 0.0, x[begin : begin + width])
            for k in range(width):
                acc = acc - columns[k][begin : begin + width] * rows[k : k + 1]
            parts.append(acc)
        x = jnp.concatenate(parts, axis=0)
    return x, jnp.log(pivots)


def coupling_inverse(directions, owned):
    number = directions.shape[1]
    row, col = iota((number, number), 0), iota((number, number), 1)
    if owned > 1:
        devices = number // owned
        source = lax.rem(col, devices) * owned + col // devices
        directions = dot(directions, jnp.where(row == source, 1.0, 0.0))
    cosines = lax.dot_general(
        directions, directions, (((0,), (0,)), ((), ())), precision=highest, preferred_element_type=jnp.float32
    )
    cosines = jnp.clip(cosines, -1.0, 1.0)
    spread = jnp.where(row == col, 1.0, 0.5 * (1.0 - cosines))
    curve = 1.5 * spread * jnp.log(spread) - 0.25 * spread + 0.5
    x = jnp.where(row == col, 1.0, curve)
    if number == SIDE:
        return invert_pair(jnp.concatenate([x, x], axis=1), PANEL)[0]
    tiles = number // SIDE
    for b in range(tiles):
        lo, hi = b * SIDE, (b + 1) * SIDE
        block = x[lo:hi, lo:hi]
        inverse = invert_pair(jnp.concatenate([block, block], axis=1), PANEL)[0][:, :SIDE]
        across = dot(inverse, x[lo:hi, :])
        down = x[:, lo:hi]
        inside_row = (row >= lo) & (row < hi)
        inside_col = (col >= lo) & (col < hi)
        updated = x - dot(down, across)
        placed = -dot(down, inverse)
        updated = jnp.where(inside_col, jnp.concatenate([placed] * tiles, axis=1), updated)
        fixed = jnp.where(
            inside_col,
            jnp.concatenate([jnp.concatenate([inverse] * tiles, axis=1)] * tiles, axis=0),
            jnp.concatenate([across] * tiles, axis=0),
        )
        x = jnp.where(inside_row, fixed, updated)
    return x


def reduce_kernel(
    chips, partial_ref, directions_ref, out_ref, coupling_ref, near_ref, sum_ref, far_ref, pad_ref,
    near_send, near_recv, far_send, far_recv
):
    me = lax.axis_index("toa")
    core = lax.rem(me, 2)
    chip = me // 2
    other = 1 - core
    owned = out_ref.shape[0]
    barrier = pltpu.get_barrier_semaphore()
    pl.semaphore_signal(barrier, inc=1, device_id={"toa": chip * 2 + other}, device_id_type=MESH)
    for d in range(1, chips):
        target = lax.rem(chip + d, chips) * 2 + core
        pl.semaphore_signal(barrier, inc=1, device_id={"toa": target}, device_id_type=MESH)
    pl.semaphore_wait(barrier, chips)
    order = [d % chips for d in range(1, chips + 1)]
    near, far = {}, {}
    for d in order:
        owner = lax.rem(chip + d, chips) * 2 + other
        for i in range(owned):
            near[d, i] = pltpu.make_async_remote_copy(
                src_ref=partial_ref.at[owner * owned + i],
                dst_ref=near_ref.at[d * owned + i],
                send_sem=near_send.at[d * owned + i],
                recv_sem=near_recv.at[d * owned + i],
                device_id={"toa": chip * 2 + other},
                device_id_type=MESH,
            )
            near[d, i].start()
    for d in order:
        owner = lax.rem(chip + d, chips) * 2 + core
        for i in range(owned):
            at = d * owned + i
            near[d, i].wait_recv()
            both = partial_ref[owner * owned + i] + near_ref[at]
            if d == 0:
                out_ref[i] = both
                continue
            sum_ref[at - owned] = both
            far[d, i] = pltpu.make_async_remote_copy(
                src_ref=sum_ref.at[at - owned],
                dst_ref=far_ref.at[at - owned],
                send_sem=far_send.at[at - owned],
                recv_sem=far_recv.at[at - owned],
                device_id={"toa": owner},
                device_id_type=MESH,
            )
            far[d, i].start()
    pad_ref[...] = jnp.zeros_like(pad_ref)
    pad_ref[0 : directions_ref.shape[0], :] = directions_ref[...]
    coupling_ref[...] = coupling_inverse(pad_ref[...], owned)
    for (d, i), copy in far.items():
        copy.wait_recv()
        out_ref[i] += far_ref[d * owned + i - owned]
    for copy in list(near.values()) + list(far.values()):
        copy.wait_send()


def reduce_owners(partial, directions, toa_devices):
    pulsars, height, lanes = partial.shape
    number = directions.shape[1]
    owned = pulsars // toa_devices
    chips = toa_devices // 2
    moved = owned * (chips - 1)
    block = (height, lanes)
    vmem = pl.BlockSpec(memory_space=pltpu.VMEM)
    return pl.pallas_call(
        functools.partial(reduce_kernel, chips),
        out_shape=(
            jax.ShapeDtypeStruct((owned,) + block, jnp.float32),
            jax.ShapeDtypeStruct((number, LANES), jnp.float32),
        ),
        in_specs=[vmem, vmem],
        out_specs=(vmem, vmem),
        scratch_shapes=[
            pltpu.VMEM((owned * chips,) + block, jnp.float32),
            pltpu.VMEM((moved,) + block, jnp.float32),
            pltpu.VMEM((moved,) + block, jnp.float32),
            pltpu.VMEM((8, number), jnp.float32),
            pltpu.SemaphoreType.DMA((owned * chips,)),
            pltpu.SemaphoreType.DMA((owned * chips,)),
            pltpu.SemaphoreType.DMA((moved,)),
            pltpu.SemaphoreType.DMA((moved,)),
        ],
        compiler_params=pltpu.CompilerParams(collective_id=0, has_side_effects=True),
        cost_estimate=pl.CostEstimate(flops=4 * pulsars * height * lanes, bytes_accessed=40 * pulsars * height * lanes, transcendentals=0),
        name="reduce_owners",
    )(partial, directions)


def paired(block):
    side, lanes = block.shape
    left = iota((side, lanes), 1) < side
    return jnp.concatenate([jnp.where(left, block, 0.0), jnp.where(left, 0.0, block)], axis=0)


def dot_paired(a, block):
    return dot(a, paired(block))


def dot_paired_t(a, block):
    return lax.dot_general(
        a, paired(block), (((1,), (1,)), ((), ())), precision=highest, preferred_element_type=jnp.float32
    )


def halves(row, side):
    left = iota(row.shape, 1) < side
    return [
        jnp.sum(jnp.where(left, row, 0.0), axis=1, keepdims=True),
        jnp.sum(jnp.where(left, 0.0, row), axis=1, keepdims=True),
    ]


def payload_rows(owned):
    return -(-17 * owned // 8) * 8


def eliminate_kernel(devices, toa_devices, sums_ref, prior_ref, coupling_ref, spectrum_ref, packed_ref, facts_ref):
    owned, height, lanes = sums_ref.shape
    side = SIDE
    columns = height - 8
    blocks = columns // side
    device = lax.axis_index("psr") * toa_devices + lax.axis_index("toa")
    lane = iota((1, lanes), 1)
    left = lane < side
    row2 = iota((side, lanes), 0)
    col2 = lax.rem(iota((side, lanes), 1), side)
    freqs = spectrum_ref.shape[1]
    pick = jnp.where(iota((freqs, lanes), 0) == lax.rem(iota((freqs, lanes), 1), side) // 2, 1.0, 0.0)
    power2 = dot(jnp.broadcast_to(1.0 / spectrum_ref[...], (8, freqs)), pick)[0:1]
    row1, col1 = iota((lanes, lanes), 0), iota((lanes, lanes), 1)
    packed_ref[...] = jnp.zeros_like(packed_ref)
    for first in range(0, owned, 2):
        pair = (first, min(first + 1, owned - 1))
        whole = []
        for p in pair:
            mixed = sums_ref[p, 0:lanes, :]
            turned = jnp.transpose(mixed)
            diag = sums_ref[p, columns + 4 : columns + 5, :]
            top = jnp.where(row1 >= col1, mixed, turned)
            low = jnp.where(row1 < col1, mixed, jnp.where(row1 == col1, diag, turned))
            whole.append({(0, 0): top, (0, 1): sums_ref[p, lanes : 2 * lanes, :], (1, 1): low})

        def join(parts, j):
            if j % 2 == 0:
                return jnp.where(left, parts[0], pltpu.roll(parts[1], side, 1))
            return jnp.where(left, pltpu.roll(parts[0], side, 1), parts[1])

        def both(i, j):
            lo = (i % 2) * side
            return join([w[i // 2, j // 2][lo : lo + side] for w in whole], j)

        order = list(range(blocks - 1, -1, -1))
        a = {}
        for s, j in enumerate(order):
            for i in order[s:]:
                a[i, j] = both(i, j)
            at = columns + j // 2
            a["p", j] = join([jnp.broadcast_to(sums_ref[p, at : at + 1, :], (8, lanes)) for p in pair], j)
            if j:
                own = jnp.concatenate([1.0 / prior_ref[p : p + 1, (j - 1) * side : j * side] for p in pair], axis=1)
                a[j, j] = a[j, j] + jnp.where(row2 == col2, own, 0.0)
        logs = jnp.zeros((1, lanes), jnp.float32)
        quads = jnp.zeros((1, lanes), jnp.float32)
        for s, j in enumerate(order[:-1]):
            inverse, extra_logs = invert_pair(a[j, j], PANEL)
            logs = logs + extra_logs
            rest = order[s + 1 :]
            scaled = {i: dot_paired(a[i, j], inverse) for i in rest + ["p"]}
            quads = quads + scaled["p"][0:1] * a["p", j][0:1]
            for t, m in enumerate(rest):
                for i in rest[t:] + ["p"]:
                    a[i, m] = a[i, m] - dot_paired_t(scaled[i], a[m, j])
        owns = []
        for h, p in enumerate(pair):
            at = (p * devices) + device
            line = coupling_ref[pl.ds(at, 1), :]
            here = lane == at
            owns.append(jnp.sum(jnp.where(here, line, 0.0), axis=1, keepdims=True))
        own2 = jnp.where(left, owns[0], owns[1])
        x, extra_logs = invert_pair(a[0, 0] + jnp.where(row2 == col2, own2 * power2, 0.0), PANEL)
        logs = halves(logs + extra_logs, side)
        quads = halves(quads, side)
        row3, col3 = row2[:HALF], col2[:HALF]
        bottom = pltpu.roll(x[HALF:], lanes - HALF, 1)
        packed = jnp.where((col3 < HALF) & (row3 < col3), bottom, x[:HALF])
        diag = jnp.sum(jnp.where(row3 + HALF == col3, x[HALF:], 0.0), axis=0, keepdims=True)
        target = a["p", 0][0:1]
        turned = pltpu.roll(packed, side, 1)
        quarter = HALF // 2
        for h, p in enumerate(pair[: min(2, owned - first)]):
            tail = sums_ref[p, columns + 2 : columns + 4, :]
            energy = jnp.sum(tail[0:1], axis=1, keepdims=True)
            count = jnp.sum(tail[1:2], axis=1, keepdims=True)
            if h == 0:
                mine = jnp.where(left, packed[:quarter], turned[quarter:])
                line = jnp.where(left, target, pltpu.roll(diag, HALF, 1))
            else:
                mine = jnp.where(left, turned[:quarter], packed[quarter:])
                line = jnp.where(left, pltpu.roll(target, side, 1), pltpu.roll(diag, lanes - HALF, 1))
            packed_ref[p * quarter : (p + 1) * quarter, :] = mine
            at = owned * quarter + p
            packed_ref[at : at + 1, :] = line
            facts = jnp.where(lane == side, logs[h] / columns, line)
            facts = jnp.where(lane == side + 1, energy - quads[h], facts)
            facts = jnp.where(lane == side + 2, count, facts)
            facts_ref[p : p + 1, :] = facts


def eliminate(sums, own_prior, coupling, spectrum, devices, toa_devices):
    owned, height, lanes = sums.shape
    return pl.pallas_call(
        functools.partial(eliminate_kernel, devices, toa_devices),
        out_shape=(
            jax.ShapeDtypeStruct((payload_rows(owned), lanes), jnp.float32),
            jax.ShapeDtypeStruct((owned, lanes), jnp.float32),
        ),
        name="eliminate",
    )(sums, own_prior, coupling, spectrum)


def total(x):
    return jnp.sum(jnp.sum(x, axis=0, keepdims=True), axis=1, keepdims=True)


def split(x):
    high = x.astype(jnp.bfloat16)
    return high, (x - high.astype(jnp.float32)).astype(jnp.bfloat16)


def conjugate(all_ref, coupling_ref, spectrum_ref, turned_ref, blocks_ref, w_ref, devices, owned):
    number = devices * owned
    rows = payload_rows(owned)
    quarter = HALF // 2
    fold = LANES // number

    def across(at):
        parts = [all_ref[pl.ds(begin, devices, stride=rows), :] for begin in at]
        return jnp.transpose(jnp.concatenate(parts * fold, axis=0))

    def turn(r, carry):
        x = across([h * quarter + r for h in range(owned)])
        turned_ref[pl.ds(pl.multiple_of(r * SIDE, SIDE), SIDE), :] = x[:SIDE]
        turned_ref[pl.ds(pl.multiple_of((r + quarter) * SIDE, SIDE), SIDE), :] = x[SIDE:]
        return carry

    for r in range(quarter):
        turn(r, 0)
    x = across([owned * quarter + h for h in range(owned)])
    target, diag = x[:SIDE], x[SIDE : SIDE + HALF]
    left = iota((HALF, LANES), 1) < SIDE
    sub = iota((HALF, LANES), 0)

    for r in range(HALF):
        mine = turned_ref[r * SIDE : r * SIDE + HALF, :]
        beside = turned_ref[r * SIDE + HALF : (r + 1) * SIDE, :]
        mirror = turned_ref[pl.ds(r, HALF, stride=SIDE), :]
        below = turned_ref[pl.ds(r + HALF, HALF, stride=SIDE), :]
        first = jnp.where(sub <= r, mine, mirror)
        last = jnp.where(sub > r, mine, jnp.where(sub == r, diag, mirror))
        if fold == 2:
            blocks_ref[r, 0:HALF, :] = jnp.where(left, first, below)
            blocks_ref[r, HALF:SIDE, :] = jnp.where(left, beside, last)
        else:
            blocks_ref[r, 0:HALF, :] = first
            blocks_ref[r, HALF:SIDE, :] = beside
            blocks_ref[r + HALF, 0:HALF, :] = below
            blocks_ref[r + HALF, HALF:SIDE, :] = last

    coupling = coupling_ref[...]
    row, col = iota(coupling.shape, 0), iota(coupling.shape, 1)
    high, low = split(jnp.where(row == lax.rem(col, number), 0.0, coupling))
    freqs = spectrum_ref.shape[1]
    place = jnp.where(iota((SIDE, freqs), 0) // 2 == iota((SIDE, freqs), 1), 1.0 / spectrum_ref[...], 0.0)
    power = dot(place, jnp.ones((freqs, LANES), jnp.float32))
    wide = iota((SIDE, LANES), 1) < SIDE

    def mix(v):
        top, rest = split(v)
        if fold == 2:
            x = jnp.where(wide, top.astype(jnp.float32), rest.astype(jnp.float32)).astype(jnp.bfloat16)
            out = jnp.dot(
                jnp.concatenate([x, x], axis=1),
                jnp.concatenate([high, high, low, low], axis=0),
                preferred_element_type=jnp.float32,
            )
        else:
            x = jnp.concatenate([top, rest], axis=1)
            out = jnp.dot(x, jnp.concatenate([high, high], axis=0), preferred_element_type=jnp.float32)
            out = out + jnp.dot(x, jnp.concatenate([low, low], axis=0), preferred_element_type=jnp.float32)
        return power * out

    def apply_blocks(v):
        if fold == 2:
            w_ref[0:HALF, :] = jnp.where(left, v[:HALF], v[HALF:])
        else:
            w_ref[...] = v
        acc = jnp.zeros((SIDE, LANES), jnp.float32)
        for k in range(SIDE // fold):
            acc = acc + blocks_ref[k] * w_ref[k : k + 1, :]
        return acc + pltpu.roll(acc, SIDE, 1) if fold == 2 else acc

    residual = target
    scaled = apply_blocks(residual)
    inner = total(residual * scaled)
    mixed = mix(scaled)
    solved = apply_blocks(mixed)
    direction, block_direction = scaled, residual
    solution = jnp.zeros((SIDE, LANES), jnp.float32)
    for iteration in range(ITERS):
        mapped = block_direction + mixed
        step = inner / total(direction * mapped)
        solution = solution + step * direction
        if iteration + 1 == ITERS:
            break
        residual = residual - step * mapped
        scaled = scaled - step * (direction + solved)
        following = total(residual * scaled)
        ratio = following / inner
        fresh = mix(scaled)
        if iteration + 2 < ITERS:
            solved = apply_blocks(fresh) + ratio * solved
        mixed = fresh + ratio * mixed
        direction = scaled + ratio * direction
        block_direction = residual + ratio * block_direction
        inner = following
    return solution


def gather_kernel(
    groups, chips, mine_ref, coupling_ref, spectrum_ref, facts_ref, out_ref, logs_ref, chi_ref,
    all_ref, turned_ref, blocks_ref, w_ref, final_ref, psr_send, chip_send, core_send, recv
):
    psr, me = lax.axis_index("psr"), lax.axis_index("toa")
    toa_devices = 2 * chips
    devices = groups * toa_devices
    core = lax.rem(me, 2)
    chip = me // 2
    other = 1 - core
    partner = chip * 2 + other
    rows = mine_ref.shape[0]
    owned = out_ref.shape[0]
    barrier = pltpu.get_barrier_semaphore()

    def greet(psr_to, toa_to):
        pl.semaphore_signal(barrier, inc=1, device_id={"psr": psr_to, "toa": toa_to}, device_id_type=MESH)

    greet(psr, partner)
    for d in range(1, chips):
        greet(psr, lax.rem(chip + d, chips) * 2 + core)
    for e in range(1, groups):
        greet(lax.rem(psr + e, groups), me)
    pl.semaphore_wait(barrier, chips + groups - 1)
    sent = []

    def block_of(e, toa):
        return lax.rem(psr + groups - e, groups) * toa_devices + toa

    def slot(block):
        return all_ref.at[pl.ds(pl.multiple_of(block * rows, 8), rows)]

    def copy(source, block, sem, psr_to, toa_to):
        return pltpu.make_async_remote_copy(
            src_ref=source,
            dst_ref=slot(block),
            send_sem=sem,
            recv_sem=recv.at[block],
            device_id={"psr": psr_to, "toa": toa_to},
            device_id_type=MESH,
        )

    def send(source, block, sem, psr_to, toa_to):
        moving = copy(source, block, sem, psr_to, toa_to)
        moving.start()
        sent.append(moving)

    def arrived(block):
        copy(slot(block), block, core_send.at[0], psr, partner).wait_recv()

    own = psr * toa_devices + me
    for e in range(1, groups):
        send(mine_ref, own, psr_send.at[e - 1], lax.rem(psr + e, groups), me)
    for e in range(groups):
        block = block_of(e, me)
        if e:
            arrived(block)
        source = slot(block) if e else mine_ref
        for d in range(1, chips):
            send(source, block, chip_send.at[e * (chips - 1) + d - 1], psr, lax.rem(chip + d, chips) * 2 + core)
        send(source, block, core_send.at[e], psr, partner)
    for d in range(1, chips):
        for e in range(groups):
            block = block_of(e, lax.rem(chip + chips - d, chips) * 2 + core)
            arrived(block)
            send(slot(block), block, core_send.at[d * groups + e], psr, partner)
    all_ref[pl.ds(pl.multiple_of(own * rows, 8), rows), :] = mine_ref[...]
    for c in range(chips):
        for e in range(groups):
            arrived(block_of(e, c * 2 + other))
    for moving in sent:
        moving.wait_send()
    solution = conjugate(all_ref, coupling_ref, spectrum_ref, turned_ref, blocks_ref, w_ref, devices, owned)
    final_ref[...] = jnp.transpose(jnp.concatenate([solution, solution], axis=0))
    lane = iota((1, LANES), 1)
    for h in range(owned):
        mine = final_ref[pl.ds(h * devices + own, 1), :]
        out_ref[h : h + 1, :] = mine[:, :SIDE]
        facts = facts_ref[h : h + 1, :]
        fit = jnp.sum(jnp.where(lane < SIDE, facts * mine, 0.0), axis=1, keepdims=True)

        def at(k):
            return jnp.sum(jnp.where(lane == SIDE + k, facts, 0.0), axis=1, keepdims=True)

        logs_ref[h : h + 1, :] = jnp.broadcast_to(at(0), (1, LANES))
        chi_ref[h : h + 1, :] = jnp.broadcast_to((at(1) - fit) / at(2), (1, LANES))


def finish(mine, coupling, spectrum, facts, groups, toa_devices):
    chips = toa_devices // 2
    devices = groups * toa_devices
    rows = mine.shape[0]
    owned = facts.shape[0]
    fold = LANES // (devices * owned)
    vmem = pl.BlockSpec(memory_space=pltpu.VMEM)
    return pl.pallas_call(
        functools.partial(gather_kernel, groups, chips),
        out_shape=(
            jax.ShapeDtypeStruct((owned, SIDE), jnp.float32),
            jax.ShapeDtypeStruct((owned, LANES), jnp.float32),
            jax.ShapeDtypeStruct((owned, LANES), jnp.float32),
        ),
        in_specs=[vmem] * 4,
        out_specs=(vmem,) * 3,
        scratch_shapes=[
            pltpu.VMEM((devices * rows, LANES), jnp.float32),
            pltpu.VMEM((HALF * SIDE, LANES), jnp.float32),
            pltpu.VMEM((SIDE // fold, SIDE, LANES), jnp.float32),
            pltpu.VMEM((SIDE, LANES), jnp.float32),
            pltpu.VMEM((LANES, LANES), jnp.float32),
            pltpu.SemaphoreType.DMA((groups - 1,)),
            pltpu.SemaphoreType.DMA((groups * (chips - 1),)),
            pltpu.SemaphoreType.DMA((groups * chips,)),
            pltpu.SemaphoreType.DMA((devices,)),
        ],
        compiler_params=pltpu.CompilerParams(collective_id=1, has_side_effects=True),
        name="finish",
    )(mine, coupling, spectrum, facts)


def body(design, noise_weight, residuals, slot_pulsar, slot_rows, own_prior, spectrum, directions):
    groups, toa_devices = lax.axis_size("psr"), lax.axis_size("toa")
    partial = local_grams(design, noise_weight, residuals, slot_pulsar, slot_rows)
    sums, coupling = reduce_owners(partial, directions, toa_devices)
    spectrum = spectrum[None, :]
    packed, facts = eliminate(sums, own_prior, coupling, spectrum, groups * toa_devices, toa_devices)
    coeffs, log_dets, chi_square = finish(packed, coupling, spectrum, facts, groups, toa_devices)
    return (coeffs, log_dets[:, 0], chi_square[:, 0])


def solution(mesh):
    return jax.shard_map(
        body,
        mesh=mesh,
        in_specs=(
            P(("psr", "toa"), None, None),
            P(("psr", "toa"), None),
            P(("psr", "toa"), None),
            P(("psr", "toa")),
            P(("psr", "toa")),
            P(("psr", "toa"), None),
            P(),
            P(),
        ),
        out_specs=(P(("psr", "toa"), None), P(("psr", "toa")), P(("psr", "toa"))),
        check_vma=False,
    )
```

time: 102 us -> 55.5 us (0.54)
  Pallas kernels: 95.6 us -> 52 us
  other arithmetic: 1.88 us -> 0 us
    pallas_call x5 -> x3, Pallas kernels: 82.7 us -> 42.2 us  [the longest x1 18.8 us: finish(): pl.pallas_call(functools.partial(gather_kernel, groups, chips), out_shape...]
    pallas_call x1, Pallas kernels: 12.9 us -> 9.71 us  [local_grams(): pl.pallas_call(gram_kernel, grid_spec=pltpu.PrefetchScalarGridSpec(num_sc...]
    reduce_sum x1 -> x0, other arithmetic: 1.36 us -> none  [body(): jnp.sum(extra[:, :common] * solution, axis=1)]
    div x2 -> x0, local copies, waits for them, and re-layouts: 1.3 us -> none  [body(): power = 1.0 / jnp.repeat(spectrum, 2)]
    unnamed x8 -> x1, local copies, waits for them, and re-layouts: 0.01 us -> 1.21 us
where the time goes in v2:
time: 55.5 us; the launch traced here: 55.2 us
  Pallas kernels  52 us (94%)
  local copies, waits for them, and re-layouts  2.55 us (5%)
  between operations  0.65 us (1%)
    pallas_call x1, Pallas kernels, finish(): pl.pallas_call(functools.partial(gather_kernel, groups, chips), out_shape...  18.8 us
    pallas_call x1, Pallas kernels, reduce_owners(): pl.pallas_call(functools.partial(reduce_kernel, chips), out_shape=(jax.Sh...  13.2 us
    pallas_call x1, Pallas kernels, eliminate(): pl.pallas_call(functools.partial(eliminate_kernel, devices, toa_devices),...  10.2 us
    pallas_call x1, Pallas kernels, local_grams(): pl.pallas_call(gram_kernel, grid_spec=pltpu.PrefetchScalarGridSpec(num_sc...  9.71 us
    slice x1, local copies, waits for them, and re-layouts, body(): return (coeffs, log_dets[:, 0], chi_square[:, 0])  1.33 us
    unnamed x1, local copies, waits for them, and re-layouts  1.21 us

profile of v2, /device:TPU:0, one launch (start us, length us, event | category | flops | bytes accessed | tf_op | source)
XLA Modules:
  0.0 55.2 jit_solution(10132486386147065379)
XLA Ops:
  0.6 9.7 %gram.1.partial_ref = f32[8,264,128]{2,1,0:T(8,128)} custom-call(s32[96]{0:T(128)} %pulsar_ref.1, s32[96]{0:T(128)} %rows_ref.1, bf16[96,128,256]{2,1,0:T(8,128)(2,1)} %design_ref.1, f32[96,128]{1,0:T(8,128)} %weight_ref.1, bf16[96,128]{1,0:T(8,128)(2,1)} %residual_ref.1), custom_call_target="tpu_custom_call" | custom-call | tf_op jit(solution)/shard_map/gram/pallas_call | solution.py:82
  10.3 13.2 %reduce_owners.1 = (f32[2,264,128]{2,1,0:T(8,128)}, f32[64,128]{1,0:T(8,128)}) custom-call(f32[8,264,128]{2,1,0:T(8,128)} %gram.1.partial_ref, f32[3,64]{1,0:T(4,128)} %directions_ref.1), custom_call_target="tpu_custom_call" | custom-call | flops 1081344 | bytes 10813440 | tf_op jit(solution)/shard_map/reduce_owners/pallas_call | solution.py:240
  23.5 10.2 %eliminate.1 = (f32[40,128]{1,0:T(8,128)}, f32[2,128]{1,0:T(2,128)}) custom-call(f32[2,264,128]{2,1,0:T(8,128)} %get-tuple-element.10.sums_ref, f32[2,192]{1,0:T(2,128)} %prior_ref.1, f32[64,128]{1,0:T(8,128)} %get-tuple-element.11.coupling_ref, f32[1,32]{1,0:T(1,128)} %bitcast.1), custom_call_target="tpu_custom_call" | custom-call | tf_op jit(solution)/shard_map/eliminate/pallas_call | solution.py:386
  33.8 18.8 %finish.1 = (f32[2,64]{1,0:T(2,128)}, f32[2,128]{1,0:T(2,128)}, f32[2,128]{1,0:T(2,128)}) custom-call(f32[40,128]{1,0:T(8,128)} %get-tuple-element.12.mine_ref, f32[64,128]{1,0:T(8,128)} %get-tuple-element.11.coupling_ref, f32[1,32]{1,0:T(1,128)} %bitcast.2, f32[2,128]{1,0:T(2,128)} %get-tuple-element.13.facts_ref), custom_call_target="tpu_custom_call" | custom-call | tf_op jit(solution)/shard_map/finish/pallas_call | solution.py:599
  52.6 1.3 %slice_reduce_fusion = (f32[2]{0:T(128)}, f32[2]{0:T(128)}) fusion(f32[2,128]{1,0:T(2,128)} %get-tuple-element.16, f32[2,128]{1,0:T(2,128)} %get-tuple-element.15), kind=kLoop, calls=%fused_computation | loop fusion | bytes 32 | tf_op jit(solution)/shard_map/slice | solution.py:631
  53.9 1.2 %copy.12 = f32[2,64]{1,0:T(2,128)} copy(f32[2,64]{1,0:T(2,128)} %get-tuple-element.22) | data formatting | bytes 1024

commit v3 on v2

--- a/solution.py
+++ b/solution.py
@@ -289,12 +289,11 @@
     return -(-17 * owned // 8) * 8
 
 
-def eliminate_kernel(devices, toa_devices, sums_ref, prior_ref, coupling_ref, spectrum_ref, packed_ref, facts_ref):
+def eliminate(devices, device, sums_ref, prior_ref, coupling_ref, spectrum_ref, packed_ref, facts_ref):
     owned, height, lanes = sums_ref.shape
     side = SIDE
     columns = height - 8
     blocks = columns // side
-    device = lax.axis_index("psr") * toa_devices + lax.axis_index("toa")
     lane = iota((1, lanes), 1)
     left = lane < side
     row2 = iota((side, lanes), 0)
@@ -381,18 +380,6 @@
             facts_ref[p : p + 1, :] = facts
 
 
-def eliminate(sums, own_prior, coupling, spectrum, devices, toa_devices):
-    owned, height, lanes = sums.shape
-    return pl.pallas_call(
-        functools.partial(eliminate_kernel, devices, toa_devices),
-        out_shape=(
-            jax.ShapeDtypeStruct((payload_rows(owned), lanes), jnp.float32),
-            jax.ShapeDtypeStruct((owned, lanes), jnp.float32),
-        ),
-        name="eliminate",
-    )(sums, own_prior, coupling, spectrum)
-
-
 def total(x):
     return jnp.sum(jnp.sum(x, axis=0, keepdims=True), axis=1, keepdims=True)
 
@@ -502,8 +489,8 @@
 
 
 def gather_kernel(
-    groups, chips, mine_ref, coupling_ref, spectrum_ref, facts_ref, out_ref, logs_ref, chi_ref,
-    all_ref, turned_ref, blocks_ref, w_ref, final_ref, psr_send, chip_send, core_send, recv
+    groups, chips, sums_ref, prior_ref, coupling_ref, spectrum_ref, out_ref,
+    mine_ref, facts_ref, all_ref, turned_ref, blocks_ref, w_ref, final_ref, psr_send, chip_send, core_send, recv
 ):
     psr, me = lax.axis_index("psr"), lax.axis_index("toa")
     toa_devices = 2 * chips
@@ -524,6 +511,8 @@
         greet(psr, lax.rem(chip + d, chips) * 2 + core)
     for e in range(1, groups):
         greet(lax.rem(psr + e, groups), me)
+    own = psr * toa_devices + me
+    eliminate(devices, own, sums_ref, prior_ref, coupling_ref, spectrum_ref, mine_ref, facts_ref)
     pl.semaphore_wait(barrier, chips + groups - 1)
     sent = []
 
@@ -551,7 +540,6 @@
     def arrived(block):
         copy(slot(block), block, core_send.at[0], psr, partner).wait_recv()
 
-    own = psr * toa_devices + me
     for e in range(1, groups):
         send(mine_ref, own, psr_send.at[e - 1], lax.rem(psr + e, groups), me)
     for e in range(groups):
@@ -578,34 +566,32 @@
     lane = iota((1, LANES), 1)
     for h in range(owned):
         mine = final_ref[pl.ds(h * devices + own, 1), :]
-        out_ref[h : h + 1, :] = mine[:, :SIDE]
         facts = facts_ref[h : h + 1, :]
         fit = jnp.sum(jnp.where(lane < SIDE, facts * mine, 0.0), axis=1, keepdims=True)
 
         def at(k):
             return jnp.sum(jnp.where(lane == SIDE + k, facts, 0.0), axis=1, keepdims=True)
 
-        logs_ref[h : h + 1, :] = jnp.broadcast_to(at(0), (1, LANES))
-        chi_ref[h : h + 1, :] = jnp.broadcast_to((at(1) - fit) / at(2), (1, LANES))
-
-
-def finish(mine, coupling, spectrum, facts, groups, toa_devices):
+        chi_square = (at(1) - fit) / at(2)
+        line = jnp.where(lane < SIDE, mine, jnp.where(lane == SIDE, at(0), chi_square))
+        out_ref[h : h + 1, :] = line
+
+
+def finish(sums, own_prior, coupling, spectrum, groups, toa_devices):
     chips = toa_devices // 2
     devices = groups * toa_devices
-    rows = mine.shape[0]
-    owned = facts.shape[0]
+    owned = sums.shape[0]
+    rows = payload_rows(owned)
     fold = LANES // (devices * owned)
     vmem = pl.BlockSpec(memory_space=pltpu.VMEM)
     return pl.pallas_call(
         functools.partial(gather_kernel, groups, chips),
-        out_shape=(
-            jax.ShapeDtypeStruct((owned, SIDE), jnp.float32),
-            jax.ShapeDtypeStruct((owned, LANES), jnp.float32),
-            jax.ShapeDtypeStruct((owned, LANES), jnp.float32),
-        ),
+        out_shape=jax.ShapeDtypeStruct((owned, LANES), jnp.float32),
         in_specs=[vmem] * 4,
-        out_specs=(vmem,) * 3,
+        out_specs=vmem,
         scratch_shapes=[
+            pltpu.VMEM((rows, LANES), jnp.float32),
+            pltpu.VMEM((owned, LANES), jnp.float32),
             pltpu.VMEM((devices * rows, LANES), jnp.float32),
             pltpu.VMEM((HALF * SIDE, LANES), jnp.float32),
             pltpu.VMEM((SIDE // fold, SIDE, LANES), jnp.float32),
@@ -618,17 +604,15 @@
         ],
         compiler_params=pltpu.CompilerParams(collective_id=1, has_side_effects=True),
         name="finish",
-    )(mine, coupling, spectrum, facts)
+    )(sums, own_prior, coupling, spectrum)
 
 
 def body(design, noise_weight, residuals, slot_pulsar, slot_rows, own_prior, spectrum, directions):
     groups, toa_devices = lax.axis_size("psr"), lax.axis_size("toa")
     partial = local_grams(design, noise_weight, residuals, slot_pulsar, slot_rows)
     sums, coupling = reduce_owners(partial, directions, toa_devices)
-    spectrum = spectrum[None, :]
-    packed, facts = eliminate(sums, own_prior, coupling, spectrum, groups * toa_devices, toa_devices)
-    coeffs, log_dets, chi_square = finish(packed, coupling, spectrum, facts, groups, toa_devices)
-    return (coeffs, log_dets[:, 0], chi_square[:, 0])
+    lines = finish(sums, own_prior, coupling, spectrum[None, :], groups, toa_devices)
+    return (lines[:, :SIDE], lines[:, SIDE], lines[:, SIDE + 1])
 
 
 def solution(mesh):

time: 55.5 us -> 53.2 us (0.959)
  Pallas kernels: 52 us -> 49.4 us
    pallas_call x1 -> x0, Pallas kernels: 10.2 us -> none  [eliminate(): pl.pallas_call(functools.partial(eliminate_kernel, devices, toa_devices),...]
    pallas_call x1, Pallas kernels: 18.8 us -> 26.6 us  [finish(): pl.pallas_call(functools.partial(gather_kernel, groups, chips), out_shape...]
where the time goes in v3:
time: 53.2 us; the launch traced here: 52.8 us
  Pallas kernels  49.4 us (93%)
  local copies, waits for them, and re-layouts  2.73 us (5%)
  between operations  0.65 us (1%)
    pallas_call x1, Pallas kernels, finish(): pl.pallas_call(functools.partial(gather_kernel, groups, chips), out_shape...  26.6 us
    pallas_call x1, Pallas kernels, reduce_owners(): pl.pallas_call(functools.partial(reduce_kernel, chips), out_shape=(jax.Sh...  13.1 us
    pallas_call x1, Pallas kernels, local_grams(): pl.pallas_call(gram_kernel, grid_spec=pltpu.PrefetchScalarGridSpec(num_sc...  9.73 us
    slice x1, local copies, waits for them, and re-layouts, body(): return (lines[:, :SIDE], lines[:, SIDE], lines[:, SIDE + 1])  1.49 us
    unnamed x1, local copies, waits for them, and re-layouts  1.24 us

profile of v3, /device:TPU:0, one launch (start us, length us, event | category | flops | bytes accessed | tf_op | source)
XLA Modules:
  0.0 52.8 jit_solution(11736281136166030527)
XLA Ops:
  0.6 9.7 %gram.1.partial_ref = f32[8,264,128]{2,1,0:T(8,128)} custom-call(s32[96]{0:T(128)} %pulsar_ref.1, s32[96]{0:T(128)} %rows_ref.1, bf16[96,128,256]{2,1,0:T(8,128)(2,1)} %design_ref.1, f32[96,128]{1,0:T(8,128)} %weight_ref.1, bf16[96,128]{1,0:T(8,128)(2,1)} %residual_ref.1), custom_call_target="tpu_custom_call" | custom-call | tf_op jit(solution)/shard_map/gram/pallas_call | solution.py:82
  10.4 13.1 %reduce_owners.1 = (f32[2,264,128]{2,1,0:T(8,128)}, f32[64,128]{1,0:T(8,128)}) custom-call(f32[8,264,128]{2,1,0:T(8,128)} %gram.1.partial_ref, f32[3,64]{1,0:T(4,128)} %directions_ref.1), custom_call_target="tpu_custom_call" | custom-call | flops 1081344 | bytes 10813440 | tf_op jit(solution)/shard_map/reduce_owners/pallas_call | solution.py:240
  23.4 26.6 %finish.1 = f32[2,128]{1,0:T(2,128)} custom-call(f32[2,264,128]{2,1,0:T(8,128)} %get-tuple-element.5.sums_ref, f32[2,192]{1,0:T(2,128)} %prior_ref.1, f32[64,128]{1,0:T(8,128)} %get-tuple-element.6.coupling_ref, f32[1,32]{1,0:T(1,128)} %bitcast.3), custom_call_target="tpu_custom_call" | custom-call | tf_op jit(solution)/shard_map/finish/pallas_call | solution.py:587
  50.0 1.5 %slice_reduce_fusion = (f32[2]{0:T(128)}, f32[2]{0:T(128)}) fusion(f32[2,128]{1,0:T(2,128)} %finish.1), kind=kLoop, calls=%fused_computation | loop fusion | bytes 32 | tf_op jit(solution)/shard_map/slice | solution.py:615
  51.5 1.2 %copy.12 = f32[2,64]{1,0:T(2,128)} copy(f32[2,64]{1,0:T(2,128)} %bitcast.2) | data formatting | bytes 1024

commit v4 on v3

--- a/solution.py
+++ b/solution.py
@@ -12,7 +12,8 @@
 SIDE = 64
 HALF = 32
 LANES = 128
-STEP_SLOTS = 16
+STEP_SLOTS = 32
+CHUNK_SLOTS = 8
 PANEL = 16
 highest = lax.Precision.HIGHEST
 MESH = pl.DeviceIdType.MESH
@@ -26,73 +27,88 @@
     return lax.broadcasted_iota(jnp.int32, shape, axis)
 
 
-def gram_kernel(pulsar_ref, rows_ref, design_ref, weight_ref, residual_ref, out_ref, acc_ref):
-    step = pl.program_id(0)
-    toas, columns = design_ref.shape[1], design_ref.shape[2]
+def gram_kernel(pulsar_ref, rows_ref, design_ref, weight_ref, residual_ref, out_ref, acc_ref, acc2_ref, held_ref, sems):
+    slots, toas, columns = design_ref.shape
     half = columns // 2
-
-    @pl.when(step == 0)
-    def _():
-        acc_ref[...] = jnp.zeros_like(acc_ref)
-
+    chunks = slots // CHUNK_SLOTS
+
+    def chunk(c):
+        at = pl.ds(pl.multiple_of(c * CHUNK_SLOTS, CHUNK_SLOTS), CHUNK_SLOTS)
+        return pltpu.make_async_copy(design_ref.at[at], held_ref.at[at], sems.at[c])
+
+    for c in range(chunks):
+        chunk(c).start()
+    acc_ref[...] = jnp.zeros_like(acc_ref)
+    acc2_ref[...] = jnp.zeros_like(acc2_ref)
     lanes = iota((1, toas), 1)
     at_row = iota((8, half), 0)
-    for j in range(STEP_SLOTS):
-        slot = step * STEP_SLOTS + j
-        p = pulsar_ref[slot]
-        valid = lanes < rows_ref[slot]
-        weight = jnp.where(valid, weight_ref[j : j + 1, :], 0.0)
-        residual = residual_ref[j : j + 1, :].astype(jnp.float32)
-        block = design_ref[j]
-        across = jnp.transpose(block).astype(jnp.float32)
-        weighted = (across * weight).astype(jnp.bfloat16)
-        gram = jnp.dot(weighted, block, preferred_element_type=jnp.float32)
-        spread = jnp.broadcast_to(residual, (8, toas)).astype(jnp.bfloat16)
-        fitted = lax.dot_general(
-            spread, weighted, (((1,), (1,)), ((), ())), preferred_element_type=jnp.float32
-        )
-        energy = weight * residual * residual
-        count = jnp.where(valid, 1.0, 0.0)
-        extra = jnp.where(at_row == 0, fitted[:, :half], jnp.where(at_row == 1, fitted[:, half:], 0.0))
-        extra = jnp.where(at_row == 2, energy, jnp.where(at_row == 3, count, extra))
-        acc_ref[p, 0:half, :] += gram[:half, :half]
-        acc_ref[p, half:columns, :] += gram[:half, half:]
-        acc_ref[p, columns : columns + half, :] += gram[half:, half:]
-        acc_ref[p, columns + half : columns + half + 8, :] += extra
-
-    @pl.when(step == pl.num_programs(0) - 1)
-    def _():
-        row, col = iota((half, half), 0), iota((half, half), 1)
-
-        def pack(p, carry):
-            low = acc_ref[p, columns : columns + half, :]
-            out_ref[p, 0:half, :] = jnp.where(row >= col, acc_ref[p, 0:half, :], low)
-            out_ref[p, half:columns, :] = acc_ref[p, half:columns, :]
-            diag = jnp.sum(jnp.where(row == col, low, 0.0), axis=0, keepdims=True)
-            tail = acc_ref[p, columns + half : columns + half + 8, :]
-            out_ref[p, columns : columns + 8, :] = jnp.where(at_row == 4, diag, tail)
-            return carry
-
-        lax.fori_loop(0, GROUP_PULSARS, pack, 0)
+
+    def step(s, carry):
+        for c in range(STEP_SLOTS // CHUNK_SLOTS):
+            chunk(s * (STEP_SLOTS // CHUNK_SLOTS) + c).wait()
+        base = pl.multiple_of(s * STEP_SLOTS, STEP_SLOTS)
+        weights = weight_ref[pl.ds(base, STEP_SLOTS), :]
+        residuals = residual_ref[pl.ds(base, STEP_SLOTS), :].astype(jnp.float32)
+        for j in range(STEP_SLOTS):
+            slot = base + j
+            p = pulsar_ref[slot]
+            into = acc_ref if j % 2 == 0 else acc2_ref
+            valid = lanes < rows_ref[slot]
+            weight = jnp.where(valid, weights[j : j + 1, :], 0.0)
+            residual = residuals[j : j + 1, :]
+            block = held_ref[slot]
+            across = jnp.transpose(block).astype(jnp.float32)
+            weighted = (across * weight).astype(jnp.bfloat16)
+            gram = jnp.dot(weighted, block, preferred_element_type=jnp.float32)
+            spread = jnp.broadcast_to(residual, (8, toas)).astype(jnp.bfloat16)
+            fitted = lax.dot_general(
+                spread, weighted, (((1,), (1,)), ((), ())), preferred_element_type=jnp.float32
+            )
+            energy = weight * residual * residual
+            count = jnp.where(valid, 1.0, 0.0)
+            extra = jnp.where(at_row == 0, fitted[:, :half], jnp.where(at_row == 1, fitted[:, half:], 0.0))
+            extra = jnp.where(at_row == 2, energy, jnp.where(at_row == 3, count, extra))
+            into[p, 0:half, :] += gram[:half, :half]
+            into[p, half:columns, :] += gram[:half, half:]
+            into[p, columns : columns + half, :] += gram[half:, half:]
+            into[p, columns + half : columns + half + 8, :] += extra
+        return carry
+
+    lax.fori_loop(0, slots // STEP_SLOTS, step, 0)
+    row, col = iota((half, half), 0), iota((half, half), 1)
+
+    def both(p, lo, hi):
+        return acc_ref[p, lo:hi, :] + acc2_ref[p, lo:hi, :]
+
+    def pack(p, carry):
+        low = both(p, columns, columns + half)
+        out_ref[p, 0:half, :] = jnp.where(row >= col, both(p, 0, half), low)
+        out_ref[p, half + 8 : columns + 8, :] = both(p, half, columns)
+        diag = jnp.sum(jnp.where(row == col, low, 0.0), axis=0, keepdims=True)
+        tail = both(p, columns + half, columns + half + 8)
+        out_ref[p, half : half + 8, :] = jnp.where(at_row == 4, diag, tail)
+        return carry
+
+    lax.fori_loop(0, GROUP_PULSARS, pack, 0)
 
 
 def local_grams(design, noise_weight, residuals, slot_pulsar, slot_rows):
     slots, toas, columns = design.shape
     half = columns // 2
+    smem = pl.BlockSpec(memory_space=pltpu.SMEM)
+    vmem = pl.BlockSpec(memory_space=pltpu.VMEM)
     return pl.pallas_call(
         gram_kernel,
-        grid_spec=pltpu.PrefetchScalarGridSpec(
-            num_scalar_prefetch=2,
-            grid=(slots // STEP_SLOTS,),
-            in_specs=[
-                pl.BlockSpec((STEP_SLOTS, toas, columns), lambda i, *_: (i, 0, 0)),
-                pl.BlockSpec((STEP_SLOTS, toas), lambda i, *_: (i, 0)),
-                pl.BlockSpec((STEP_SLOTS, toas), lambda i, *_: (i, 0)),
-            ],
-            out_specs=pl.BlockSpec((GROUP_PULSARS, columns + 8, half), lambda i, *_: (0, 0, 0)),
-            scratch_shapes=[pltpu.VMEM((GROUP_PULSARS, columns + half + 8, half), jnp.float32)],
-        ),
-        out_shape=jax.ShapeDtypeStruct((GROUP_PULSARS, columns + 8, half), jnp.float32),
+        in_specs=[smem, smem, pl.BlockSpec(memory_space=pltpu.HBM), vmem, vmem],
+        out_specs=vmem,
+        out_shape=pltpu.VMEM((GROUP_PULSARS, columns + 8, half), jnp.float32),
+        scratch_shapes=[
+            pltpu.VMEM((GROUP_PULSARS, columns + half + 8, half), jnp.float32),
+            pltpu.VMEM((GROUP_PULSARS, columns + half + 8, half), jnp.float32),
+            pltpu.VMEM((slots, toas, columns), jnp.bfloat16),
+            pltpu.SemaphoreType.DMA((slots // CHUNK_SLOTS,)),
+        ],
+        compiler_params=pltpu.CompilerParams(vmem_limit_bytes=54 * 2**20),
         name="gram",
     )(slot_pulsar, slot_rows, design, noise_weight, residuals)
 
@@ -171,65 +187,147 @@
     return x
 
 
+def paired(block):
+    side, lanes = block.shape
+    left = iota((side, lanes), 1) < side
+    return jnp.concatenate([jnp.where(left, block, 0.0), jnp.where(left, 0.0, block)], axis=0)
+
+
+def dot_paired(a, block):
+    return dot(a, paired(block))
+
+
+def dot_paired_t(a, block):
+    return lax.dot_general(
+        a, paired(block), (((1,), (1,)), ((), ())), precision=highest, preferred_element_type=jnp.float32
+    )
+
+
+def halves(row, side):
+    left = iota(row.shape, 1) < side
+    return [
+        jnp.sum(jnp.where(left, row, 0.0), axis=1, keepdims=True),
+        jnp.sum(jnp.where(left, 0.0, row), axis=1, keepdims=True),
+    ]
+
+
+def unpack(mixed, diag, upper):
+    row, col = iota(mixed.shape, 0), iota(mixed.shape, 1)
+    turned = jnp.transpose(mixed)
+    if upper:
+        return jnp.where(row >= col, mixed, turned)
+    return jnp.where(row < col, mixed, jnp.where(row == col, diag, turned))
+
+
+def join(parts, j, side):
+    left = iota(parts[0].shape, 1) < side
+    if j % 2 == 0:
+        return jnp.where(left, parts[0], pltpu.roll(parts[1], side, 1))
+    return jnp.where(left, pltpu.roll(parts[0], side, 1), parts[1])
+
+
+def with_prior(block, prior_ref, pair, j):
+    side, lanes = block.shape
+    row, col = iota((side, lanes), 0), lax.rem(iota((side, lanes), 1), side)
+    own = jnp.concatenate([1.0 / prior_ref[p : p + 1, (j - 1) * side : j * side] for p in pair], axis=1)
+    return block + jnp.where(row == col, own, 0.0)
+
+
+def pair_of(first, owned):
+    return (first, min(first + 1, owned - 1))
+
+
 def reduce_kernel(
-    chips, partial_ref, directions_ref, out_ref, coupling_ref, near_ref, sum_ref, far_ref, pad_ref,
+    chips, partial_ref, directions_ref, prior_ref, out_ref, coupling_ref, early_ref, near_ref, sum_ref, far_ref, pad_ref,
     near_send, near_recv, far_send, far_recv
 ):
     me = lax.axis_index("toa")
     core = lax.rem(me, 2)
     chip = me // 2
     other = 1 - core
-    owned = out_ref.shape[0]
+    owned, height, lanes = out_ref.shape
+    side = SIDE
+    pieces = ((side, lanes + 8), (0, side), (lanes + 8, height))
     barrier = pltpu.get_barrier_semaphore()
     pl.semaphore_signal(barrier, inc=1, device_id={"toa": chip * 2 + other}, device_id_type=MESH)
     for d in range(1, chips):
         target = lax.rem(chip + d, chips) * 2 + core
         pl.semaphore_signal(barrier, inc=1, device_id={"toa": target}, device_id_type=MESH)
     pl.semaphore_wait(barrier, chips)
-    order = [d % chips for d in range(1, chips + 1)]
+    order = [(d % chips, i, q) for d in range(1, chips) for q in range(3) for i in range(owned)]
+    order += [(0, i, q) for q in range(3) for i in range(owned)]
     near, far = {}, {}
-    for d in order:
+    for d, i, q in order:
         owner = lax.rem(chip + d, chips) * 2 + other
-        for i in range(owned):
-            near[d, i] = pltpu.make_async_remote_copy(
-                src_ref=partial_ref.at[owner * owned + i],
-                dst_ref=near_ref.at[d * owned + i],
-                send_sem=near_send.at[d * owned + i],
-                recv_sem=near_recv.at[d * owned + i],
-                device_id={"toa": chip * 2 + other},
-                device_id_type=MESH,
-            )
-            near[d, i].start()
-    for d in order:
+        at, (lo, hi) = d * owned + i, pieces[q]
+        near[d, i, q] = pltpu.make_async_remote_copy(
+            src_ref=partial_ref.at[owner * owned + i, lo:hi],
+            dst_ref=near_ref.at[at, lo:hi],
+            send_sem=near_send.at[at, q],
+            recv_sem=near_recv.at[at, q],
+            device_id={"toa": chip * 2 + other},
+            device_id_type=MESH,
+        )
+        near[d, i, q].start()
+    for d, i, q in order:
         owner = lax.rem(chip + d, chips) * 2 + core
-        for i in range(owned):
-            at = d * owned + i
-            near[d, i].wait_recv()
-            both = partial_ref[owner * owned + i] + near_ref[at]
-            if d == 0:
-                out_ref[i] = both
-                continue
-            sum_ref[at - owned] = both
-            far[d, i] = pltpu.make_async_remote_copy(
-                src_ref=sum_ref.at[at - owned],
-                dst_ref=far_ref.at[at - owned],
-                send_sem=far_send.at[at - owned],
-                recv_sem=far_recv.at[at - owned],
-                device_id={"toa": owner},
-                device_id_type=MESH,
-            )
-            far[d, i].start()
+        at, (lo, hi) = d * owned + i, pieces[q]
+        near[d, i, q].wait_recv()
+        both = partial_ref[owner * owned + i, lo:hi] + near_ref[at, lo:hi]
+        if d == 0:
+            out_ref[i, lo:hi] = both
+            continue
+        sum_ref[at - owned, lo:hi] = both
+        far[d, i, q] = pltpu.make_async_remote_copy(
+            src_ref=sum_ref.at[at - owned, lo:hi],
+            dst_ref=far_ref.at[at - owned, lo:hi],
+            send_sem=far_send.at[at - owned, q],
+            recv_sem=far_recv.at[at - owned, q],
+            device_id={"toa": owner},
+            device_id_type=MESH,
+        )
+        far[d, i, q].start()
     pad_ref[...] = jnp.zeros_like(pad_ref)
     pad_ref[0 : directions_ref.shape[0], :] = directions_ref[...]
     coupling_ref[...] = coupling_inverse(pad_ref[...], owned)
-    for (d, i), copy in far.items():
-        copy.wait_recv()
-        out_ref[i] += far_ref[d * owned + i - owned]
+
+    def collect(q):
+        lo, hi = pieces[q]
+        for d, i, which in order:
+            if d and which == q:
+                far[d, i, q].wait_recv()
+                out_ref[i, lo:hi] += far_ref[(d - 1) * owned + i, lo:hi]
+
+    pairs = [pair_of(first, owned) for first in range(0, owned, 2)]
+    corner = lax.broadcasted_iota(jnp.int32, (side, lanes), 0) - iota((side, lanes), 1) + side
+    collect(0)
+    firsts = []
+    for n, pair in enumerate(pairs):
+        parts = []
+        for p in pair:
+            mixed, diag = out_ref[p, side:lanes], out_ref[p, lanes + 4 : lanes + 5]
+            turned = jnp.transpose(jnp.concatenate([mixed, mixed], axis=0))[side:]
+            turned = jnp.concatenate([turned[:, :side], turned[:, :side]], axis=1)
+            parts.append(jnp.where(corner < 0, mixed, jnp.where(corner == 0, diag, turned)))
+        inverse, logs = invert_pair(with_prior(join(parts, 1, side), prior_ref, pair, 3), PANEL)
+        early_ref[n, 0:side, :] = inverse
+        firsts.append((inverse, logs))
+    collect(1)
+    for n, pair in enumerate(pairs):
+        low = [unpack(out_ref[p, 0:lanes], out_ref[p, lanes + 4 : lanes + 5], False) for p in pair]
+        inverse, logs = firsts[n]
+        cross = join([x[:side] for x in low], 1, side)
+        before = with_prior(join([x[:side] for x in low], 0, side), prior_ref, pair, 2)
+        scaled = dot_paired(cross, inverse)
+        inverse, more = invert_pair(before - dot_paired_t(scaled, cross), PANEL)
+        early_ref[n, side : 2 * side, :] = inverse
+        early_ref[n, 2 * side :, :] = jnp.broadcast_to(logs + more, (8, lanes))
+    collect(2)
     for copy in list(near.values()) + list(far.values()):
         copy.wait_send()
 
 
-def reduce_owners(partial, directions, toa_devices):
+def reduce_owners(partial, directions, own_prior, toa_devices):
     pulsars, height, lanes = partial.shape
     number = directions.shape[1]
     owned = pulsars // toa_devices
@@ -242,54 +340,31 @@
         out_shape=(
             jax.ShapeDtypeStruct((owned,) + block, jnp.float32),
             jax.ShapeDtypeStruct((number, LANES), jnp.float32),
+            jax.ShapeDtypeStruct(((owned + 1) // 2, 2 * SIDE + 8, LANES), jnp.float32),
         ),
-        in_specs=[vmem, vmem],
-        out_specs=(vmem, vmem),
+        in_specs=[vmem] * 3,
+        out_specs=(vmem,) * 3,
         scratch_shapes=[
             pltpu.VMEM((owned * chips,) + block, jnp.float32),
             pltpu.VMEM((moved,) + block, jnp.float32),
             pltpu.VMEM((moved,) + block, jnp.float32),
             pltpu.VMEM((8, number), jnp.float32),
-            pltpu.SemaphoreType.DMA((owned * chips,)),
-            pltpu.SemaphoreType.DMA((owned * chips,)),
-            pltpu.SemaphoreType.DMA((moved,)),
-            pltpu.SemaphoreType.DMA((moved,)),
+            pltpu.SemaphoreType.DMA((owned * chips, 3)),
+            pltpu.SemaphoreType.DMA((owned * chips, 3)),
+            pltpu.SemaphoreType.DMA((moved, 3)),
+            pltpu.SemaphoreType.DMA((moved, 3)),
         ],
-        compiler_params=pltpu.CompilerParams(collective_id=0, has_side_effects=True),
+        compiler_params=pltpu.CompilerParams(collective_id=0, has_side_effects=True, vmem_limit_bytes=20 * 2**20),
         cost_estimate=pl.CostEstimate(flops=4 * pulsars * height * lanes, bytes_accessed=40 * pulsars * height * lanes, transcendentals=0),
         name="reduce_owners",
-    )(partial, directions)
-
-
-def paired(block):
-    side, lanes = block.shape
-    left = iota((side, lanes), 1) < side
-    return jnp.concatenate([jnp.where(left, block, 0.0), jnp.where(left, 0.0, block)], axis=0)
-
-
-def dot_paired(a, block):
-    return dot(a, paired(block))
-
-
-def dot_paired_t(a, block):
-    return lax.dot_general(
-        a, paired(block), (((1,), (1,)), ((), ())), precision=highest, preferred_element_type=jnp.float32
-    )
-
-
-def halves(row, side):
-    left = iota(row.shape, 1) < side
-    return [
-        jnp.sum(jnp.where(left, row, 0.0), axis=1, keepdims=True),
-        jnp.sum(jnp.where(left, 0.0, row), axis=1, keepdims=True),
-    ]
+    )(partial, directions, own_prior)
 
 
 def payload_rows(owned):
     return -(-17 * owned // 8) * 8
 
 
-def eliminate(devices, device, sums_ref, prior_ref, coupling_ref, spectrum_ref, packed_ref, facts_ref):
+def eliminate(devices, device, sums_ref, early_ref, prior_ref, coupling_ref, spectrum_ref, packed_ref, facts_ref):
     owned, height, lanes = sums_ref.shape
     side = SIDE
     columns = height - 8
@@ -301,43 +376,39 @@
     freqs = spectrum_ref.shape[1]
     pick = jnp.where(iota((freqs, lanes), 0) == lax.rem(iota((freqs, lanes), 1), side) // 2, 1.0, 0.0)
     power2 = dot(jnp.broadcast_to(1.0 / spectrum_ref[...], (8, freqs)), pick)[0:1]
-    row1, col1 = iota((lanes, lanes), 0), iota((lanes, lanes), 1)
     packed_ref[...] = jnp.zeros_like(packed_ref)
     for first in range(0, owned, 2):
-        pair = (first, min(first + 1, owned - 1))
+        pair = pair_of(first, owned)
         whole = []
         for p in pair:
-            mixed = sums_ref[p, 0:lanes, :]
-            turned = jnp.transpose(mixed)
-            diag = sums_ref[p, columns + 4 : columns + 5, :]
-            top = jnp.where(row1 >= col1, mixed, turned)
-            low = jnp.where(row1 < col1, mixed, jnp.where(row1 == col1, diag, turned))
-            whole.append({(0, 0): top, (0, 1): sums_ref[p, lanes : 2 * lanes, :], (1, 1): low})
-
-        def join(parts, j):
-            if j % 2 == 0:
-                return jnp.where(left, parts[0], pltpu.roll(parts[1], side, 1))
-            return jnp.where(left, pltpu.roll(parts[0], side, 1), parts[1])
+            mixed, diag = sums_ref[p, 0:lanes, :], sums_ref[p, lanes + 4 : lanes + 5, :]
+            whole.append({
+                (0, 0): unpack(mixed, diag, True),
+                (0, 1): sums_ref[p, lanes + 8 : 2 * lanes + 8, :],
+                (1, 1): unpack(mixed, diag, False),
+            })
 
         def both(i, j):
             lo = (i % 2) * side
-            return join([w[i // 2, j // 2][lo : lo + side] for w in whole], j)
+            return join([w[i // 2, j // 2][lo : lo + side] for w in whole], j, side)
 
         order = list(range(blocks - 1, -1, -1))
         a = {}
         for s, j in enumerate(order):
             for i in order[s:]:
                 a[i, j] = both(i, j)
-            at = columns + j // 2
-            a["p", j] = join([jnp.broadcast_to(sums_ref[p, at : at + 1, :], (8, lanes)) for p in pair], j)
-            if j:
-                own = jnp.concatenate([1.0 / prior_ref[p : p + 1, (j - 1) * side : j * side] for p in pair], axis=1)
-                a[j, j] = a[j, j] + jnp.where(row2 == col2, own, 0.0)
-        logs = jnp.zeros((1, lanes), jnp.float32)
+            at = lanes + j // 2
+            a["p", j] = join([jnp.broadcast_to(sums_ref[p, at : at + 1, :], (8, lanes)) for p in pair], j, side)
+        a[1, 1] = with_prior(a[1, 1], prior_ref, pair, 1)
+        early = early_ref.at[first // 2]
+        logs = early[2 * side : 2 * side + 1, :]
         quads = jnp.zeros((1, lanes), jnp.float32)
         for s, j in enumerate(order[:-1]):
-            inverse, extra_logs = invert_pair(a[j, j], PANEL)
-            logs = logs + extra_logs
+            if s < 2:
+                inverse = early[s * side : (s + 1) * side, :]
+            else:
+                inverse, extra_logs = invert_pair(a[j, j], PANEL)
+                logs = logs + extra_logs
             rest = order[s + 1 :]
             scaled = {i: dot_paired(a[i, j], inverse) for i in rest + ["p"]}
             quads = quads + scaled["p"][0:1] * a["p", j][0:1]
@@ -362,7 +433,7 @@
         turned = pltpu.roll(packed, side, 1)
         quarter = HALF // 2
         for h, p in enumerate(pair[: min(2, owned - first)]):
-            tail = sums_ref[p, columns + 2 : columns + 4, :]
+            tail = sums_ref[p, lanes + 2 : lanes + 4, :]
             energy = jnp.sum(tail[0:1], axis=1, keepdims=True)
             count = jnp.sum(tail[1:2], axis=1, keepdims=True)
             if h == 0:
@@ -489,7 +560,7 @@
 
 
 def gather_kernel(
-    groups, chips, sums_ref, prior_ref, coupling_ref, spectrum_ref, out_ref,
+    groups, chips, sums_ref, early_ref, prior_ref, coupling_ref, spectrum_ref, out_ref,
     mine_ref, facts_ref, all_ref, turned_ref, blocks_ref, w_ref, final_ref, psr_send, chip_send, core_send, recv
 ):
     psr, me = lax.axis_index("psr"), lax.axis_index("toa")
@@ -512,7 +583,7 @@
     for e in range(1, groups):
         greet(lax.rem(psr + e, groups), me)
     own = psr * toa_devices + me
-    eliminate(devices, own, sums_ref, prior_ref, coupling_ref, spectrum_ref, mine_ref, facts_ref)
+    eliminate(devices, own, sums_ref, early_ref, prior_ref, coupling_ref, spectrum_ref, mine_ref, facts_ref)
     pl.semaphore_wait(barrier, chips + groups - 1)
     sent = []
 
@@ -577,7 +648,7 @@
         out_ref[h : h + 1, :] = line
 
 
-def finish(sums, own_prior, coupling, spectrum, groups, toa_devices):
+def finish(sums, early, own_prior, coupling, spectrum, groups, toa_devices):
     chips = toa_devices // 2
     devices = groups * toa_devices
     owned = sums.shape[0]
@@ -587,7 +658,7 @@
     return pl.pallas_call(
         functools.partial(gather_kernel, groups, chips),
         out_shape=jax.ShapeDtypeStruct((owned, LANES), jnp.float32),
-        in_specs=[vmem] * 4,
+        in_specs=[vmem] * 5,
         out_specs=vmem,
         scratch_shapes=[
             pltpu.VMEM((rows, LANES), jnp.float32),
@@ -602,16 +673,16 @@
             pltpu.SemaphoreType.DMA((groups * chips,)),
             pltpu.SemaphoreType.DMA((devices,)),
         ],
-        compiler_params=pltpu.CompilerParams(collective_id=1, has_side_effects=True),
+        compiler_params=pltpu.CompilerParams(collective_id=1, has_side_effects=True, vmem_limit_bytes=20 * 2**20),
         name="finish",
-    )(sums, own_prior, coupling, spectrum)
+    )(sums, early, own_prior, coupling, spectrum)
 
 
 def body(design, noise_weight, residuals, slot_pulsar, slot_rows, own_prior, spectrum, directions):
     groups, toa_devices = lax.axis_size("psr"), lax.axis_size("toa")
     partial = local_grams(design, noise_weight, residuals, slot_pulsar, slot_rows)
-    sums, coupling = reduce_owners(partial, directions, toa_devices)
-    lines = finish(sums, own_prior, coupling, spectrum[None, :], groups, toa_devices)
+    sums, coupling, early = reduce_owners(partial, directions, own_prior, toa_devices)
+    lines = finish(sums, early, own_prior, coupling, spectrum[None, :], groups, toa_devices)
     return (lines[:, :SIDE], lines[:, SIDE], lines[:, SIDE + 1])
 
 

time: 53.2 us -> 43.2 us (0.81)
  Pallas kernels: 49.4 us -> 40.9 us
  local copies, waits for them, and re-layouts: 2.73 us -> 1.3 us
    pallas_call x1, Pallas kernels: 26.6 us -> 22 us  [finish(): pl.pallas_call(functools.partial(gather_kernel, groups, chips), out_shape...]
    pallas_call x1, Pallas kernels: 13.1 us -> 11.1 us  [reduce_owners(): pl.pallas_call(functools.partial(reduce_kernel, chips), out_shape=(jax.Sh...]
    pallas_call x1, Pallas kernels: 9.73 us -> 7.79 us  [local_grams(): pl.pallas_call(gram_kernel, in_specs=[smem, smem, pl.BlockSpec(memory_spa...]
    slice x1, local copies, waits for them, and re-layouts: 1.49 us -> 0.73 us  [body(): return (lines[:, :SIDE], lines[:, SIDE], lines[:, SIDE + 1])]
    unnamed x1 -> x7, local copies, waits for them, and re-layouts: 1.24 us -> 0.57 us
where the time goes in v4:
time: 43.2 us; the launch traced here: 42.9 us
  Pallas kernels  40.9 us (95%)
  local copies, waits for them, and re-layouts  1.3 us (3%)
  between operations  0.71 us (2%)
    pallas_call x1, Pallas kernels, finish(): pl.pallas_call(functools.partial(gather_kernel, groups, chips), out_shape...  22 us
    pallas_call x1, Pallas kernels, reduce_owners(): pl.pallas_call(functools.partial(reduce_kernel, chips), out_shape=(jax.Sh...  11.1 us
    pallas_call x1, Pallas kernels, local_grams(): pl.pallas_call(gram_kernel, in_specs=[smem, smem, pl.BlockSpec(memory_spa...  7.79 us

profile of v4, /device:TPU:0, one launch (start us, length us, event | category | flops | bytes accessed | tf_op | source)
XLA Modules:
  0.0 42.9 jit_solution(9662090849597689778)
XLA Ops:
  0.6 0.0 copy-start
  0.6 0.0 copy-start.1
  0.7 0.0 copy-start.2
  0.7 7.8 %gram.1.partial_ref = f32[8,264,128]{2,1,0:T(8,128)S(1)} custom-call(s32[96]{0:T(128)} %pulsar_ref.1, s32[96]{0:T(128)} %rows_ref.1, bf16[96,128,256]{2,1,0:T(8,128)(2,1)} %design_ref.1, f32[96,128]{1,0:T(8,128)} %weight_ref.1, bf16[96,128]{1,0:T(8,128)(2,1)} %residual_ref.1), custom_call_target="tpu_custom_call" | custom-call | tf_op jit(solution)/shard_map/gram/pallas_call | solution.py:100
  8.5 0.0 copy-done
  8.5 0.0 copy-done.1
  8.5 11.1 %reduce_owners.1 = (f32[2,264,128]{2,1,0:T(8,128)S(1)}, f32[64,128]{1,0:T(8,128)S(1)}, f32[1,136,128]{2,1,0:T(8,128)S(1)}) custom-call(f32[8,264,128]{2,1,0:T(8,128)S(1)} %gram.1.partial_ref, f32[3,64]{1,0:T(4,128)S(1)} %copy-done.1, f32[2,192]{1,0:T(2,128)S(1)} %copy-done), custom_call_target="tpu_custom_call" | custom-call | flops 1081344 | bytes 10813440 | tf_op jit(solution)/shard_map/reduce_owners/pallas_call | solution.py:338
  19.6 0.0 copy-done.2
  19.6 22.0 %finish.1 = f32[2,128]{1,0:T(2,128)S(1)} custom-call(f32[2,264,128]{2,1,0:T(8,128)S(1)} %get-tuple-element.6.sums_ref, f32[1,136,128]{2,1,0:T(8,128)S(1)} %get-tuple-element.7.early_ref, f32[2,192]{1,0:T(2,128)S(1)} %copy-done, f32[64,128]{1,0:T(8,128)S(1)} %get-tuple-element.8.coupling_ref, f32[1,32]{1,0:T(1,128)S(1)} %bitcast.3), custom_call_target="tpu_custom_call" | custom-call | tf_op jit(solution)/shard_map/finish/pallas_call | solution.py:658
  41.6 0.7 %slice_reduce_fusion = (f32[2]{0:T(128)}, f32[2]{0:T(128)}) fusion(f32[2,128]{1,0:T(2,128)S(1)} %finish.1), kind=kLoop, calls=%fused_computation | loop fusion | bytes 32 | tf_op jit(solution)/shard_map/slice | solution.py:686
  42.4 0.6 %copy.12 = f32[2,64]{1,0:T(2,128)} copy(f32[2,64]{1,0:T(2,128)S(1)} %bitcast.2) | data formatting | bytes 1024
Async XLA Ops:
  0.6 7.8 %copy-start = (f32[2,192]{1,0:T(2,128)S(1)}, f32[2,192]{1,0:T(2,128)}, u32[]{:S(2)}) copy-start(f32[2,192]{1,0:T(2,128)} %prior_ref.3) | copy-start | bytes 4612
  0.6 7.8 %copy-start.1 = (f32[3,64]{1,0:T(4,128)S(1)}, f32[3,64]{1,0:T(4,128)}, u32[]{:S(2)}) copy-start(f32[3,64]{1,0:T(4,128)} %directions_ref.1) | copy-start | bytes 2308
  0.7 18.9 %copy-start.2 = (f32[32]{0:T(128)S(1)}, f32[32]{0:T(128)}, u32[]{:S(2)}) copy-start(f32[32]{0:T(128)} %param.14) | copy-start | bytes 388
